TPU v7x, 32 devices: a whole 2x2x4 slice. The times are simulated.
32 devices in a mesh: ctx: 16 (over z, y, core), tp: 2 (over x).
Axes of the slice: x: 2, y: 2, z: 4, core: 2. Of those that a mesh axis runs over, the one named last changes fastest.
Arguments:
- query_se: bfloat16 [3584, 8192], P('ctx', 'tp'), may hold values from -6 to 6
- key_se: bfloat16 [3584, 8192], P('ctx', 'tp'), may hold values from -6 to 6
- value_se: bfloat16 [3584, 8192], P('ctx', 'tp'), may hold values from -6 to 6
- query_mr: bfloat16 [3584, 8192], P('ctx', 'tp'), may hold values from -6 to 6
- key_mr: bfloat16 [3584, 8192], P('ctx', 'tp'), may hold values from -6 to 6
- upstream: bfloat16 [3584, 8192], P('ctx', 'tp'), may hold values from -6 to 6
- filter_se: float32 [7, 8192], P(None, 'tp'), may hold values from -2 to 2
- filter_mr: float32 [128, 8192], P(None, 'tp'), may hold values from -0.5 to 0.5
- skip_mr: float32 [8192], P('tp'), may hold values from -1 to 1
- norm_gain: float32 [8192], P('tp'), may hold values from 0.1 to 1.9
Outputs:
- grad_query_se: bfloat16 [3584, 8192], P('ctx', 'tp')
- grad_key_se: bfloat16 [3584, 8192], P('ctx', 'tp')
- grad_value_se: bfloat16 [3584, 8192], P('ctx', 'tp')
- grad_query_mr: bfloat16 [3584, 8192], P('ctx', 'tp')
- grad_key_mr: bfloat16 [3584, 8192], P('ctx', 'tp')
- grad_filter_se: float32 [7, 8192], P(None, ('tp', 'ctx'))
- grad_filter_mr: float32 [128, 8192], P(None, ('tp', 'ctx'))
- grad_skip: float32 [8192], P(('tp', 'ctx'))
- grad_gain: float32 [8192], P(('tp', 'ctx'))
All inputs are finite; a program needn't handle non-finite values.
Results may differ from a plain program's by a relative error of at most 0.0062.
Values may be sent and summed in bfloat16 or wider, within the bound.
A program may use at most 128 MiB of HBM per device.

v0:
```python
import functools
import math

import jax
import jax.numpy as jnp
import numpy as np
from jax import lax
from jax.experimental import pallas as pl
from jax.experimental.pallas import tpu as pltpu
from jax.sharding import PartitionSpec as P

EPSILON = 0.1
F32 = jnp.float32
BF16 = jnp.bfloat16
LANES = 128


def shifted(block, axis, distance):
    devices = range(lax.axis_size(axis))
    route = [(i - distance, i) for i in devices if i - distance in devices]
    return lax.ppermute(block, axis, route)


def transforms(rows, taps):
    length = rows + taps
    freq = 2.0 * np.pi * (np.arange(length // 2) + 0.5) / length

    def forward(start, stop):
        angle = freq[:, None] * np.arange(start, stop)[None, :]
        return np.concatenate([np.cos(angle), -np.sin(angle)], 0)

    angle = np.arange(max(rows, taps))[:, None] * freq[None, :]
    inverse = np.concatenate([np.cos(angle), -np.sin(angle)], 1) * (2.0 / length)
    mats = forward(-taps, rows), forward(0, length), forward(0, taps), inverse
    return [jnp.asarray(m, BF16) for m in mats]


def dot(a, b):
    return jnp.dot(a, b, preferred_element_type=F32)


def lane_sum(value):
    total = value[:, :LANES]
    for start in range(LANES, value.shape[1], LANES):
        total = total + value[:, start : start + LANES]
    return total


def row_scale(width, *parts):
    total = parts[0][...]
    for part in parts[1:]:
        total = total + part[...]
    return lax.rsqrt(jnp.sum(total, axis=1, keepdims=True) * (1.0 / width) + EPSILON)


def short_kernel(q_ref, k_ref, v_ref, tail_ref, f_ref, conv_ref, sq_ref, pad):
    rows, block = q_ref.shape
    halo = tail_ref.shape[0]

    @pl.when(pl.program_id(0) == 0)
    def _():
        sq_ref[...] = jnp.zeros_like(sq_ref)

    for start in range(0, block, LANES):
        cols = slice(start, start + LANES)
        pad[:halo, :] = tail_ref[:, cols].astype(F32)
        product = k_ref[:, cols].astype(F32) * v_ref[:, cols].astype(F32)
        pad[halo:, :] = product.astype(BF16).astype(F32)
        conv = f_ref[0:1, cols] * pad[pl.ds(halo, rows), :]
        for j in range(1, f_ref.shape[0]):
            conv = conv + f_ref[j : j + 1, cols] * pad[pl.ds(halo - j, rows), :]
        conv_ref[:, cols] = conv
        mixed = q_ref[:, cols].astype(F32) * conv
        sq_ref[...] += mixed * mixed


def product_kernel(width, nsq, *refs):
    sq = refs[:nsq]
    q_ref, conv_ref, km_ref, gain_ref, out_ref, tail_ref = refs[nsq:]
    scale = row_scale(width, *sq)
    halo = tail_ref.shape[0]
    for start in range(0, q_ref.shape[1], LANES):
        cols = slice(start, start + LANES)
        normed = q_ref[:, cols].astype(F32) * conv_ref[:, cols] * scale * gain_ref[:, cols]
        product = (km_ref[:, cols].astype(F32) * normed).astype(BF16)
        out_ref[:, cols] = product
        tail_ref[:, cols] = product[product.shape[0] - halo :]


def adjoint_kernel(width, nsq, *refs):
    sq = refs[:nsq]
    (up_ref, qm_ref, head_ref, f_ref, skip_ref, q_ref, conv_ref, km_ref, gain_ref,
     fg_ref, fh_ref, inv_ref, gk_ref, gn_ref, w_ref) = refs[nsq:]
    rows, block = q_ref.shape
    half = fg_ref.shape[0] // 2

    @pl.when(pl.program_id(0) == 0)
    def _():
        w_ref[...] = jnp.zeros_like(w_ref)

    g = (up_ref[...].astype(F32) * qm_ref[...].astype(F32)).astype(BF16)
    gs = dot(fg_ref[...], jnp.concatenate([g, head_ref[...]], 0))
    hs = dot(fh_ref[...], f_ref[...].astype(BF16))
    hr, hi = hs[:half] + skip_ref[...], hs[half:]
    gr, gi = gs[:half], gs[half:]
    spectrum = jnp.concatenate(
        [(gr * hr + gi * hi).astype(BF16), (gi * hr - gr * hi).astype(BF16)], 0
    )
    gp = dot(inv_ref[:rows, :], spectrum)
    scale = row_scale(width, *sq)
    for start in range(0, block, LANES):
        cols = slice(start, start + LANES)
        mixed = q_ref[:, cols].astype(F32) * conv_ref[:, cols]
        back = gp[:, cols]
        gain = gain_ref[:, cols]
        gk_ref[:, cols] = (back * (mixed * scale * gain)).astype(BF16)
        gn = back * km_ref[:, cols].astype(F32)
        gn_ref[:, cols] = gn
        w_ref[...] += gn * gain * mixed


def medium_kernel(z_ref, tail_ref, up_ref, qm_ref, f_ref, skip_ref, fz_ref, fg_ref, fh_ref,
                  inv_ref, gq_ref, corr_ref):
    rows, block = up_ref.shape
    half = fz_ref.shape[0] // 2
    taps = f_ref.shape[0]
    up = up_ref[...].astype(F32)
    g = (up * qm_ref[...].astype(F32)).astype(BF16)
    zs = dot(fz_ref[...], jnp.concatenate([tail_ref[...], z_ref[...]], 0))
    hs = dot(fh_ref[...], f_ref[...].astype(BF16))
    gs = dot(fg_ref[:, :rows], g)
    hr, hi = hs[:half] + skip_ref[...], hs[half:]
    zr, zi = zs[:half], zs[half:]
    gr, gi = gs[:half], gs[half:]
    spectrum = jnp.concatenate(
        [(zr * hr - zi * hi).astype(BF16), (zr * hi + zi * hr).astype(BF16)], 0
    )
    gq_ref[...] = (up * dot(inv_ref[:rows, :], spectrum)).astype(BF16)
    cross = jnp.concatenate(
        [(gr * zr + gi * zi).astype(BF16), (gi * zr - gr * zi).astype(BF16)], 0
    )
    corr = dot(inv_ref[:taps, :], cross)
    share = corr_ref.shape[2]
    for part in range(corr_ref.shape[0]):
        corr_ref[part] = corr[:, part * share : (part + 1) * share]


def back_kernel(width, nsq, *refs):
    sq, ws = refs[:nsq], refs[nsq : 2 * nsq]
    (q_ref, k_ref, v_ref, tail_ref, head_ref, conv_ref, gn_ref, gain_ref, f_ref,
     gq_ref, gk_ref, gv_ref, small_ref, pad_p, pad_g) = refs[2 * nsq :]
    rows, block = q_ref.shape
    halo = tail_ref.shape[0]
    taps = f_ref.shape[0]
    share = small_ref.shape[2]
    scale = row_scale(width, *sq)
    weight = ws[0][...]
    for part in ws[1:]:
        weight = weight + part[...]
    coef = jnp.sum(weight, axis=1, keepdims=True) * (scale * scale * scale) * (1.0 / width)
    for start in range(0, block, LANES):
        cols = slice(start, start + LANES)
        q = q_ref[:, cols].astype(F32)
        conv = conv_ref[:, cols]
        mixed = q * conv
        gn = gn_ref[:, cols] * scale
        gm = gain_ref[:, cols] * gn - mixed * coef
        gq_ref[:, cols] = (gm * conv).astype(BF16)
        gc = (gm * q).astype(BF16).astype(F32)
        pad_g[:rows, :] = gc
        pad_g[rows:, :] = head_ref[:, cols].astype(F32)
        part, inner = start // share, start % share
        place = slice(inner, inner + LANES)
        small_ref[part, taps : taps + 1, place] = jnp.sum(gn * mixed, axis=0, keepdims=True)
        k = k_ref[:, cols].astype(F32)
        v = v_ref[:, cols].astype(F32)
        pad_p[:halo, :] = tail_ref[:, cols].astype(F32)
        pad_p[halo:, :] = (k * v).astype(BF16).astype(F32)
        gp = f_ref[0:1, cols] * gc
        for j in range(taps):
            if j:
                gp = gp + f_ref[j : j + 1, cols] * pad_g[pl.ds(j, rows), :]
            small_ref[part, j : j + 1, place] = jnp.sum(
                gc * pad_p[pl.ds(halo - j, rows), :], axis=0, keepdims=True
            )
        gk_ref[:, cols] = (gp * v).astype(BF16)
        gv_ref[:, cols] = (gp * k).astype(BF16)


def up_to(value, step):
    return -(-value // step) * step


def split_parts(parts, share):
    count, height, group = parts.shape
    if group == share:
        return parts
    parts = parts.reshape(count, height, group // share, share)
    return parts.transpose(0, 2, 1, 3).reshape(-1, height, share)


def scatter_sum(parts, axis):
    size = lax.axis_size(axis)
    me = lax.axis_index(axis)
    bit = 1
    while bit < size:
        rest = parts.reshape((parts.shape[0] // 2, 2) + parts.shape[1:])
        mine = lax.rem(me // bit, 2)
        away = lax.dynamic_index_in_dim(rest, 1 - mine, 1, keepdims=False).astype(BF16)
        keep = lax.dynamic_index_in_dim(rest, mine, 1, keepdims=False)
        got = lax.ppermute(away, axis, [(i, i ^ bit) for i in range(size)])
        parts = keep + got.astype(F32)
        bit *= 2
    return parts[0]


def exchanged(value, axis):
    size = lax.axis_size(axis)
    others = []
    for step in range(1, size):
        others.append(lax.ppermute(value, axis, [(i, (i + step) % size) for i in range(size)]))
    return [value] + others


def local(
    query_se, key_se, value_se, query_mr, key_mr, upstream, filter_se, filter_mr, skip_mr, norm_gain
):
    rows, chans = query_se.shape
    taps_se, taps = filter_se.shape[0], filter_mr.shape[0]
    ctx = lax.axis_size("ctx")
    width = chans * lax.axis_size("tp")
    tokens = rows * ctx
    share = chans // ctx
    group = up_to(share, LANES)
    halo = up_to(taps_se - 1, 16)
    block = max(group, min(512, chans))
    steps = chans // block
    fz, fg, fh, inv = transforms(rows, taps)
    length = rows + taps
    skip = skip_mr[None]
    gain = norm_gain[None]

    def rowed(n):
        return pl.BlockSpec((n, block), lambda i: (0, i))

    def whole(a):
        return pl.BlockSpec(a.shape, lambda i: (0, 0))

    lanes_spec = pl.BlockSpec((rows, LANES), lambda i: (0, 0))
    stream = rowed(rows)
    one = rowed(1)

    def call(body, name, ins, specs, outs, out_specs, scratch=(), flops=0):
        moved = sum(a.size * a.dtype.itemsize for a in list(ins) + list(outs))
        return pl.pallas_call(
            body,
            name=name,
            grid=(steps,),
            in_specs=specs,
            out_specs=out_specs,
            out_shape=outs,
            scratch_shapes=scratch,
            cost_estimate=pl.CostEstimate(flops=flops, bytes_accessed=moved, transcendentals=0),
            compiler_params=pltpu.CompilerParams(
                dimension_semantics=("arbitrary",), vmem_limit_bytes=56 * 2**20
            ),
        )(*ins)

    def shape(n, kind):
        return jax.ShapeDtypeStruct((n, chans), kind)

    lanes_shape = jax.ShapeDtypeStruct((rows, LANES), F32)

    tail_se = shifted(
        (key_se[rows - halo :].astype(F32) * value_se[rows - halo :].astype(F32)).astype(BF16),
        "ctx", 1,
    )
    head_mr = shifted(
        (upstream[:taps].astype(F32) * query_mr[:taps].astype(F32)).astype(BF16), "ctx", -1
    )
    conv_se, squares = call(
        short_kernel, "short",
        (query_se, key_se, value_se, tail_se, filter_se),
        [stream, stream, stream, rowed(halo), rowed(taps_se)],
        [shape(rows, F32), lanes_shape], [stream, lanes_spec],
        [pltpu.VMEM((halo + rows, LANES), F32)],
    )
    sq = exchanged(squares, "tp")
    nsq = len(sq)
    product_mr, tail = call(
        functools.partial(product_kernel, width, nsq), "product",
        (*sq, query_se, conv_se, key_mr, gain),
        [lanes_spec] * nsq + [stream, stream, stream, one],
        [shape(rows, BF16), shape(taps, BF16)], [stream, rowed(taps)],
    )
    tail_mr = shifted(tail, "ctx", 1)
    grad_key_mr, grad_normed, weight = call(
        functools.partial(adjoint_kernel, width, nsq), "adjoint",
        (*sq, upstream, query_mr, head_mr, filter_mr, skip, query_se, conv_se, key_mr, gain,
         fg, fh, inv),
        [lanes_spec] * nsq
        + [stream, stream, rowed(taps), rowed(taps), one, stream, stream, stream, one,
           whole(fg), whole(fh), whole(inv)],
        [shape(rows, BF16), shape(rows, F32), lanes_shape], [stream, stream, lanes_spec],
        flops=2 * length * (length + taps + rows) * chans,
    )
    ws = exchanged(weight, "tp")
    first = slice(0, halo)
    scale = lax.rsqrt(jnp.sum(sum(a[first] for a in sq), axis=1, keepdims=True) / width + EPSILON)
    coef = scale**3 * jnp.sum(sum(a[first] for a in ws), axis=1, keepdims=True) / width
    q_head = query_se[first].astype(F32)
    mixed_head = gain * scale * grad_normed[first] - q_head * conv_se[first] * coef
    head_se = shifted((mixed_head * q_head).astype(BF16), "ctx", -1)
    grad_query_mr, corr = call(
        medium_kernel, "medium",
        (product_mr, tail_mr, upstream, query_mr, filter_mr, skip, fz, fg, fh, inv),
        [stream, rowed(taps), stream, stream, rowed(taps), one,
         whole(fz), whole(fg), whole(fh), whole(inv)],
        [shape(rows, BF16), jax.ShapeDtypeStruct((chans // group, taps, group), F32)],
        [stream, pl.BlockSpec((block // group, taps, group), lambda i: (i, 0, 0))],
        flops=2 * length * (length + taps + rows + rows + taps) * chans,
    )
    grad_query_se, grad_key_se, grad_value_se, small = call(
        functools.partial(back_kernel, width, nsq), "back",
        (*sq, *ws, query_se, key_se, value_se, tail_se, head_se, conv_se, grad_normed, gain,
         filter_se),
        [lanes_spec] * (2 * nsq)
        + [stream, stream, stream, rowed(halo), rowed(halo), stream, stream, one, rowed(taps_se)],
        [shape(rows, BF16)] * 3 + [jax.ShapeDtypeStruct((chans // group, taps_se + 1, group), F32)],
        [stream] * 3 + [pl.BlockSpec((block // group, taps_se + 1, group), lambda i: (i, 0, 0))],
        [pltpu.VMEM((halo + rows, LANES), F32), pltpu.VMEM((halo + rows, LANES), F32)],
    )
    factor = 1.0 / math.sqrt(tokens)
    corr, small = split_parts(corr, share), split_parts(small, share)
    total_mr = scatter_sum(corr, "ctx") * factor
    total = jnp.sum(lax.all_to_all(small, "ctx", 0, 0, tiled=True), axis=0) * factor
    return (
        grad_query_se,
        grad_key_se,
        grad_value_se,
        grad_query_mr,
        grad_key_mr,
        total[:taps_se],
        total_mr,
        total_mr[0],
        total[taps_se],
    )


def solution(mesh):
    streams = (P("ctx", "tp"),)
    in_specs = streams * 6 + (P(None, "tp"), P(None, "tp"), P("tp"), P("tp"))
    both = ("tp", "ctx")
    out_specs = streams * 5 + (P(None, both), P(None, both), P(both), P(both))
    return jax.shard_map(local, mesh=mesh, in_specs=in_specs, out_specs=out_specs, check_vma=False)
```

profile of v0, /device:TPU:0, one launch (start us, length us, event | category | flops | bytes accessed | tf_op | source)
XLA Modules:
  0.0 136.3 jit_solution(15214724673433812727)
XLA Ops:
  1.6 2.4 %collective-permute-start = (bf16[16,4096]{1,0:T(8,128)(2,1)S(1)}, bf16[16,4096]{1,0:T(8,128)(2,1)S(1)}, u32[]{:S(2)}, u32[]{:S(2)}) collective-permute-start(bf16[16,4096]{1,0:T(8,128)(2,1)S(1)} %multiply_convert_fusion.1), channel_id=1, source_target_pairs={{0,2},{2,4},{4,6},{6,8},{8,10},{10,12},{12,14},{14,16},{16,18},{18... | collective-permute-start | bytes 393224 | tf_op jit(solution)/shard_map/ppermute | solution.py:21
  5.7 8.6 %short.1 = (f32[224,4096]{1,0:T(8,128)}, f32[224,128]{1,0:T(8,128)}) custom-call(bf16[224,4096]{1,0:T(8,128)(2,1)} %refs_2_.3, bf16[224,4096]{1,0:T(8,128)(2,1)} %refs_5_.3, bf16[224,4096]{1,0:T(8,128)(2,1)} %refs_6_.1, bf16[16,4096]{1,0:T(8,128)(2,1)} %copy-done.5, f32[7,4096]{1,0:T(8,128)} %refs_12_.2), custom_call_target="tpu_custom_call" | custom-call | bytes 9535488 | tf_op jit(solution)/shard_map/short/pallas_call | solution.py:255
  14.3 2.3 %collective-permute-start.1 = (f32[224,128]{1,0:T(8,128)}, f32[224,128]{1,0:T(8,128)S(1)}, u32[]{:S(2)}, u32[]{:S(2)}) collective-permute-start(f32[224,128]{1,0:T(8,128)} %get-tuple-element.22.refs_0_), channel_id=1, source_target_pairs={{0,1},{1,0},{2,3},{3,2},{4,5},{5,4},{6,7},{7,6},{8,9},{9,8},{10,11... | collective-permute-start | bytes 344072 | tf_op jit(solution)/shard_map/ppermute | solution.py:221
  16.6 3.0 %collective-permute-done.1.refs_1_ = f32[224,128]{1,0:T(8,128)S(1)} collective-permute-done((f32[224,128]{1,0:T(8,128)}, f32[224,128]{1,0:T(8,128)S(1)}, u32[]{:S(2)}, u32[]{:S(2)}) %collective-permute-start.1) | collective-permute-done | bytes 114720 | tf_op jit(solution)/shard_map/ppermute | solution.py:221
  20.2 7.8 %product.1 = (bf16[224,4096]{1,0:T(8,128)(2,1)}, bf16[128,4096]{1,0:T(8,128)(2,1)}) custom-call(f32[224,128]{1,0:T(8,128)} %get-tuple-element.22.refs_0_, f32[224,128]{1,0:T(8,128)} %copy-done.3, bf16[224,4096]{1,0:T(8,128)(2,1)} %refs_2_.3, f32[224,4096]{1,0:T(8,128)} %get-tuple-element.23.refs_8_.refs_9_.refs_3_, bf16[224,4096]{1,0:T(8,128)(2,1)} %refs_4_.3, ...), custom_call_target="tpu_custom_call" | custom-call | bytes 10469376 | tf_op jit(solution)/shard_map/product/pallas_call | solution.py:255
  28.0 4.1 %collective-permute-start.5 = (bf16[128,4096]{1,0:T(8,128)(2,1)}, bf16[128,4096]{1,0:T(8,128)(2,1)S(1)}, u32[]{:S(2)}, u32[]{:S(2)}) collective-permute-start(bf16[128,4096]{1,0:T(8,128)(2,1)} %get-tuple-element.30), channel_id=1, source_target_pairs={{0,2},{2,4},{4,6},{6,8},{8,10},{10,12},{12,14},{14,16},{16,18},{18... | collective-permute-start | bytes 3145736 | tf_op jit(solution)/shard_map/ppermute | solution.py:21
  32.1 1.2 multiply_convert_fusion
  33.4 1.3 collective-permute-start.2
  35.6 11.0 %medium.1 = (bf16[224,4096]{1,0:T(8,128)(2,1)}, f32[16,128,256]{2,1,0:T(8,128)}) custom-call(bf16[224,4096]{1,0:T(8,128)(2,1)} %get-tuple-element.29.z_ref, bf16[128,4096]{1,0:T(8,128)(2,1)} %copy-done.11, bf16[224,4096]{1,0:T(8,128)(2,1)} %up_ref.1, bf16[224,4096]{1,0:T(8,128)(2,1)} %qm_ref.1, f32[128,4096]{1,0:T(8,128)} %f_ref.3, f32[1,4096]{1,0:T(1,128)} %bitcast.35, ...), custom_call_target="tpu_custom_call" | custom-call | flops 3045064704 | bytes 13342720 | tf_op jit(solution)/shard_map/medium/pallas_call | solution.py:255
  46.7 2.1 %fusion = bf16[8,128,256]{2,1,0:T(8,128)(2,1)} fusion(f32[8,2,128,256]{3,2,1,0:T(8,128)} %bitcast.29, s32[]{:T(128)S(6)} %select_n.41), kind=kLoop, calls=%fused_computation.3 | loop fusion | bytes 1048580 | tf_op jit(solution)/shard_map/convert_element_type | solution.py:209
  48.8 24.3 %collective-permute-start.6 = (bf16[8,128,256]{2,1,0:T(8,128)(2,1)}, bf16[8,128,256]{2,1,0:T(8,128)(2,1)}, u32[]{:S(2)}, u32[]{:S(2)}) collective-permute-start(bf16[8,128,256]{2,1,0:T(8,128)(2,1)} %fusion), channel_id=1, source_target_pairs={{0,2},{2,0},{4,6},{6,4},{8,10},{10,8},{12,14},{14,12},{16,18},{18,... | collective-permute-start | bytes 1572872 | tf_op jit(solution)/shard_map/ppermute | solution.py:211
  74.0 12.7 %adjoint.1 = (bf16[224,4096]{1,0:T(8,128)(2,1)}, f32[224,4096]{1,0:T(8,128)}, f32[224,128]{1,0:T(8,128)}) custom-call(f32[224,128]{1,0:T(8,128)} %get-tuple-element.22.refs_0_, f32[224,128]{1,0:T(8,128)} %copy-done.3, bf16[224,4096]{1,0:T(8,128)(2,1)} %up_ref.1, bf16[224,4096]{1,0:T(8,128)(2,1)} %qm_ref.1, bf16[128,4096]{1,0:T(8,128)(2,1)} %copy-done.4, ...), custom_call_target="tpu_custom_call" | custom-call | flops 2030043136 | bytes 20533248 | tf_op jit(solution)/shard_map/adjoint/pallas_call | solution.py:255
  86.7 1.5 %collective-permute-start.3 = (f32[224,128]{1,0:T(8,128)}, f32[224,128]{1,0:T(8,128)S(1)}, u32[]{:S(2)}, u32[]{:S(2)}) collective-permute-start(f32[224,128]{1,0:T(8,128)} %get-tuple-element.24.refs_2_), channel_id=1, source_target_pairs={{0,1},{1,0},{2,3},{3,2},{4,5},{5,4},{6,7},{7,6},{8,9},{9,8},{10,11... | collective-permute-start | bytes 344072 | tf_op jit(solution)/shard_map/ppermute | solution.py:221
  89.1 3.0 %collective-permute-done.3.refs_3_ = f32[224,128]{1,0:T(8,128)S(1)} collective-permute-done((f32[224,128]{1,0:T(8,128)}, f32[224,128]{1,0:T(8,128)S(1)}, u32[]{:S(2)}, u32[]{:S(2)}) %collective-permute-start.3) | collective-permute-done | bytes 114720 | tf_op jit(solution)/shard_map/ppermute | solution.py:221
  94.1 2.8 %collective-permute-start.7 = (bf16[4,128,256]{2,1,0:T(8,128)(2,1)S(1)}, bf16[4,128,256]{2,1,0:T(8,128)(2,1)S(1)}, u32[]{:S(2)}, u32[]{:S(2)}) collective-permute-start(bf16[4,128,256]{2,1,0:T(8,128)(2,1)S(1)} %fusion.4), channel_id=1, source_target_pairs={{0,4},{2,6},{4,0},{6,2},{8,12},{10,14},{12,8},{14,10},{16,20},{18,... | collective-permute-start | bytes 786440 | tf_op jit(solution)/shard_map/ppermute | solution.py:211
  96.9 1.2 fusion.3
  98.1 1.3 collective-permute-start.4
  99.5 1.9 %collective-permute-done.4.refs_8_ = bf16[16,4096]{1,0:T(8,128)(2,1)S(1)} collective-permute-done((bf16[16,4096]{1,0:T(8,128)(2,1)S(1)}, bf16[16,4096]{1,0:T(8,128)(2,1)S(1)}, u32[]{:S(2)}, u32[]{:S(2)}) %collective-permute-start.4) | collective-permute-done | bytes 131104 | tf_op jit(solution)/shard_map/ppermute | solution.py:21
  102.0 12.9 %back.1 = (bf16[224,4096]{1,0:T(8,128)(2,1)}, bf16[224,4096]{1,0:T(8,128)(2,1)}, bf16[224,4096]{1,0:T(8,128)(2,1)}, f32[16,8,256]{2,1,0:T(8,128)}) custom-call(f32[224,128]{1,0:T(8,128)} %get-tuple-element.22.refs_0_, f32[224,128]{1,0:T(8,128)} %copy-done.3, f32[224,128]{1,0:T(8,128)} %get-tuple-element.24.refs_2_, f32[224,128]{1,0:T(8,128)} %copy-done.8, ...), custom_call_target="tpu_custom_call" | custom-call | bytes 19333120 | tf_op jit(solution)/shard_map/back/pallas_call | solution.py:255
  115.0 6.7 %all-to-all-start = ((f32[16,8,256]{2,1,0:T(8,128)}), f32[16,8,256]{2,1,0:T(8,128)S(1)}, u32[]{:S(2)}, u32[]{:S(2)}) async-start(f32[16,8,256]{2,1,0:T(8,128)} %get-tuple-element.33), calls=%async_computation | async-start | bytes 262144 | tf_op jit(solution)/shard_map/all_to_all | solution.py:336
  121.8 2.0 %collective-permute-start.8 = (bf16[2,128,256]{2,1,0:T(8,128)(2,1)S(1)}, bf16[2,128,256]{2,1,0:T(8,128)(2,1)S(1)}, u32[]{:S(2)}, u32[]{:S(2)}) collective-permute-start(bf16[2,128,256]{2,1,0:T(8,128)(2,1)S(1)} %fusion.5), channel_id=1, source_target_pairs={{0,8},{2,10},{4,12},{6,14},{8,0},{10,2},{12,4},{14,6},{16,24},{18,... | collective-permute-start | bytes 393224 | tf_op jit(solution)/shard_map/ppermute | solution.py:211
  123.8 6.4 %all-to-all-done = f32[16,8,256]{2,1,0:T(8,128)S(1)} async-done(((f32[16,8,256]{2,1,0:T(8,128)}), f32[16,8,256]{2,1,0:T(8,128)S(1)}, u32[]{:S(2)}, u32[]{:S(2)}) %all-to-all-start) | async-done | bytes 131104 | tf_op jit(solution)/shard_map/all_to_all | solution.py:336
  130.2 1.9 %collective-permute-start.9 = (bf16[1,128,256]{2,1,0:T(8,128)(2,1)S(1)}, bf16[1,128,256]{2,1,0:T(8,128)(2,1)S(1)}, u32[]{:S(2)}, u32[]{:S(2)}) collective-permute-start(bf16[1,128,256]{2,1,0:T(8,128)(2,1)S(1)} %dynamic-slice_convert_fusion.2), channel_id=1, source_target_pairs={{0,16},{2,18},{4,20},{6,22},{8,24},{10,26},{12,28},{14,30},{16,0},... | collective-permute-start | bytes 196616 | tf_op jit(solution)/shard_map/ppermute | solution.py:211
  132.7 2.9 %collective-permute-done.9 = bf16[1,128,256]{2,1,0:T(8,128)(2,1)S(1)} collective-permute-done((bf16[1,128,256]{2,1,0:T(8,128)(2,1)S(1)}, bf16[1,128,256]{2,1,0:T(8,128)(2,1)S(1)}, u32[]{:S(2)}, u32[]{:S(2)}) %collective-permute-start.9) | collective-permute-done | bytes 65568 | tf_op jit(solution)/shard_map/ppermute | solution.py:211
  (45 shorter events, 10.1 us)
Async XLA Ops:
  1.6 3.4 %collective-permute-start = (bf16[16,4096]{1,0:T(8,128)(2,1)S(1)}, bf16[16,4096]{1,0:T(8,128)(2,1)S(1)}, u32[]{:S(2)}, u32[]{:S(2)}) collective-permute-start(bf16[16,4096]{1,0:T(8,128)(2,1)S(1)} %multiply_convert_fusion.1), channel_id=1, source_target_pairs={{0,2},{2,4},{4,6},{6,8},{8,10},{10,12},{12,14},{14,16},{16,18},{18... | collective-permute-start | bytes 393224 | tf_op jit(solution)/shard_map/ppermute | solution.py:21
  5.0 0.7 copy-start.5
  14.3 5.3 %collective-permute-start.1 = (f32[224,128]{1,0:T(8,128)}, f32[224,128]{1,0:T(8,128)S(1)}, u32[]{:S(2)}, u32[]{:S(2)}) collective-permute-start(f32[224,128]{1,0:T(8,128)} %get-tuple-element.22.refs_0_), channel_id=1, source_target_pairs={{0,1},{1,0},{2,3},{3,2},{4,5},{5,4},{6,7},{7,6},{8,9},{9,8},{10,11... | collective-permute-start | bytes 344072 | tf_op jit(solution)/shard_map/ppermute | solution.py:221
  19.5 0.6 copy-start.3
  20.2 11.9 %copy-start = (bf16[224,4096]{1,0:T(8,128)(2,1)S(1)}, bf16[224,4096]{1,0:T(8,128)(2,1)}, u32[]{:S(2)}) copy-start(bf16[224,4096]{1,0:T(8,128)(2,1)} %up_ref.1) | copy-start | bytes 5505028
  20.2 11.9 %copy-start.1 = (bf16[224,4096]{1,0:T(8,128)(2,1)S(1)}, bf16[224,4096]{1,0:T(8,128)(2,1)}, u32[]{:S(2)}) copy-start(bf16[224,4096]{1,0:T(8,128)(2,1)} %qm_ref.1) | copy-start | bytes 5505028
  28.0 6.6 %collective-permute-start.5 = (bf16[128,4096]{1,0:T(8,128)(2,1)}, bf16[128,4096]{1,0:T(8,128)(2,1)S(1)}, u32[]{:S(2)}, u32[]{:S(2)}) collective-permute-start(bf16[128,4096]{1,0:T(8,128)(2,1)} %get-tuple-element.30), channel_id=1, source_target_pairs={{0,2},{2,4},{4,6},{6,8},{8,10},{10,12},{12,14},{14,16},{16,18},{18... | collective-permute-start | bytes 3145736 | tf_op jit(solution)/shard_map/ppermute | solution.py:21
  33.4 39.6 %collective-permute-start.2 = (bf16[128,4096]{1,0:T(8,128)(2,1)}, bf16[128,4096]{1,0:T(8,128)(2,1)S(1)}, u32[]{:S(2)}, u32[]{:S(2)}) collective-permute-start(bf16[128,4096]{1,0:T(8,128)(2,1)} %multiply_convert_fusion), channel_id=1, source_target_pairs={{2,0},{4,2},{6,4},{8,6},{10,8},{12,10},{14,12},{16,14},{18,16},{20... | collective-permute-start | bytes 3145736 | tf_op jit(solution)/shard_map/ppermute | solution.py:21
  34.7 1.0 copy-start.11
  48.8 44.2 %copy-start.2 = (f32[16,128,256]{2,1,0:T(8,128)S(1)}, f32[16,128,256]{2,1,0:T(8,128)}, u32[]{:S(2)}) copy-start(f32[16,128,256]{2,1,0:T(8,128)} %get-tuple-element.34) | copy-start | bytes 6291460
  48.8 44.2 %collective-permute-start.6 = (bf16[8,128,256]{2,1,0:T(8,128)(2,1)}, bf16[8,128,256]{2,1,0:T(8,128)(2,1)}, u32[]{:S(2)}, u32[]{:S(2)}) collective-permute-start(bf16[8,128,256]{2,1,0:T(8,128)(2,1)} %fusion), channel_id=1, source_target_pairs={{0,2},{2,0},{4,6},{6,4},{8,10},{10,8},{12,14},{14,12},{16,18},{18,... | collective-permute-start | bytes 1572872 | tf_op jit(solution)/shard_map/ppermute | solution.py:211
  73.0 1.0 copy-start.4
  86.7 10.2 %copy-start.6 = (f32[4096]{0:T(1024)S(1)}, f32[4096]{0:T(1024)}, u32[]{:S(2)}) copy-start(f32[4096]{0:T(1024)} %param.23) | copy-start | bytes 49156
  86.7 5.4 %collective-permute-start.3 = (f32[224,128]{1,0:T(8,128)}, f32[224,128]{1,0:T(8,128)S(1)}, u32[]{:S(2)}, u32[]{:S(2)}) collective-permute-start(f32[224,128]{1,0:T(8,128)} %get-tuple-element.24.refs_2_), channel_id=1, source_target_pairs={{0,1},{1,0},{2,3},{3,2},{4,5},{5,4},{6,7},{7,6},{8,9},{9,8},{10,11... | collective-permute-start | bytes 344072 | tf_op jit(solution)/shard_map/ppermute | solution.py:221
  92.1 6.0 %copy-start.8 = (f32[224,128]{1,0:T(8,128)}, f32[224,128]{1,0:T(8,128)S(1)}, u32[]{:S(2)}) copy-start(f32[224,128]{1,0:T(8,128)S(1)} %collective-permute-done.3.refs_3_) | copy-start | bytes 344068
  94.1 27.5 %collective-permute-start.7 = (bf16[4,128,256]{2,1,0:T(8,128)(2,1)S(1)}, bf16[4,128,256]{2,1,0:T(8,128)(2,1)S(1)}, u32[]{:S(2)}, u32[]{:S(2)}) collective-permute-start(bf16[4,128,256]{2,1,0:T(8,128)(2,1)S(1)} %fusion.4), channel_id=1, source_target_pairs={{0,4},{2,6},{4,0},{6,2},{8,12},{10,14},{12,8},{14,10},{16,20},{18,... | collective-permute-start | bytes 786440 | tf_op jit(solution)/shard_map/ppermute | solution.py:211
  98.1 3.2 %collective-permute-start.4 = (bf16[16,4096]{1,0:T(8,128)(2,1)S(1)}, bf16[16,4096]{1,0:T(8,128)(2,1)S(1)}, u32[]{:S(2)}, u32[]{:S(2)}) collective-permute-start(bf16[16,4096]{1,0:T(8,128)(2,1)S(1)} %fusion.3), channel_id=1, source_target_pairs={{2,0},{4,2},{6,4},{8,6},{10,8},{12,10},{14,12},{16,14},{18,16},{20... | collective-permute-start | bytes 393224 | tf_op jit(solution)/shard_map/ppermute | solution.py:21
  101.4 0.6 copy-start.9
  115.0 15.2 %all-to-all-start = ((f32[16,8,256]{2,1,0:T(8,128)}), f32[16,8,256]{2,1,0:T(8,128)S(1)}, u32[]{:S(2)}, u32[]{:S(2)}) async-start(f32[16,8,256]{2,1,0:T(8,128)} %get-tuple-element.33), calls=%async_computation | async-start | bytes 262144 | tf_op jit(solution)/shard_map/all_to_all | solution.py:336
  121.8 8.4 %collective-permute-start.8 = (bf16[2,128,256]{2,1,0:T(8,128)(2,1)S(1)}, bf16[2,128,256]{2,1,0:T(8,128)(2,1)S(1)}, u32[]{:S(2)}, u32[]{:S(2)}) collective-permute-start(bf16[2,128,256]{2,1,0:T(8,128)(2,1)S(1)} %fusion.5), channel_id=1, source_target_pairs={{0,8},{2,10},{4,12},{6,14},{8,0},{10,2},{12,4},{14,6},{16,24},{18,... | collective-permute-start | bytes 393224 | tf_op jit(solution)/shard_map/ppermute | solution.py:211
  130.2 5.4 %collective-permute-start.9 = (bf16[1,128,256]{2,1,0:T(8,128)(2,1)S(1)}, bf16[1,128,256]{2,1,0:T(8,128)(2,1)S(1)}, u32[]{:S(2)}, u32[]{:S(2)}) collective-permute-start(bf16[1,128,256]{2,1,0:T(8,128)(2,1)S(1)} %dynamic-slice_convert_fusion.2), channel_id=1, source_target_pairs={{0,16},{2,18},{4,20},{6,22},{8,24},{10,26},{12,28},{14,30},{16,0},... | collective-permute-start | bytes 196616 | tf_op jit(solution)/shard_map/ppermute | solution.py:211
  132.2 4.1 %copy-start.10 = (f32[8,256]{1,0:T(8,128)}, f32[8,256]{1,0:T(8,128)S(1)}, u32[]{:S(2)}) copy-start(f32[8,256]{1,0:T(8,128)S(1)} %broadcast_multiply_fusion) | copy-start | bytes 24580
  135.7 0.7 copy-start.7
where the time goes:
time: 138 us; the launch traced here: 136 us
  Pallas kernels  53.1 us (38%)
  starting transfers between devices  50.6 us (37%)
  waiting for transfers between devices  18.1 us (13%)
  local copies, waits for them, and re-layouts  7.26 us (5%)
  other arithmetic  6.35 us (5%)
    pallas_call x5, Pallas kernels, call(): pl.pallas_call(body, name=name, grid=(steps,), in_specs=specs, out_specs=...  53.1 us
    ppermute x4, starting transfers between devices, scatter_sum(): got = lax.ppermute(away, axis, [(i, i ^ bit) for i in range(size)])  31 us
    ppermute x4, starting transfers between devices, shifted(): return lax.ppermute(block, axis, route)  9.08 us
    all_to_all x1, starting transfers between devices, local(): lax.all_to_all(small, 'ctx', 0, 0, tiled=True)  6.71 us
    all_to_all x1, waiting for transfers between devices, local(): lax.all_to_all(small, 'ctx', 0, 0, tiled=True)  6.38 us
    ppermute x2, waiting for transfers between devices, exchanged(): lax.ppermute(value, axis, [(i, (i + step) % size) for i in range(size)])  5.96 us
    unnamed x24, local copies, waits for them, and re-layouts  3.95 us
    ppermute x2, starting transfers between devices, exchanged(): lax.ppermute(value, axis, [(i, (i + step) % size) for i in range(size)])  3.86 us
  transfers between devices with their start and end apart: 11, of which 6 were waited for; matrix products, arithmetic and copies ran while one was open for 5% of the time, Pallas kernels for 27%

commit v1 on v0

--- a/solution.py
+++ b/solution.py
@@ -9,6 +9,7 @@
 from jax.experimental.pallas import tpu as pltpu
 from jax.sharding import PartitionSpec as P
 
+
 EPSILON = 0.1
 F32 = jnp.float32
 BF16 = jnp.bfloat16
@@ -37,13 +38,6 @@
 
 def dot(a, b):
     return jnp.dot(a, b, preferred_element_type=F32)
-
-
-def lane_sum(value):
-    total = value[:, :LANES]
-    for start in range(LANES, value.shape[1], LANES):
-        total = total + value[:, start : start + LANES]
-    return total
 
 
 def row_scale(width, *parts):
@@ -74,90 +68,83 @@
         sq_ref[...] += mixed * mixed
 
 
-def product_kernel(width, nsq, *refs):
-    sq = refs[:nsq]
-    q_ref, conv_ref, km_ref, gain_ref, out_ref, tail_ref = refs[nsq:]
-    scale = row_scale(width, *sq)
-    halo = tail_ref.shape[0]
-    for start in range(0, q_ref.shape[1], LANES):
-        cols = slice(start, start + LANES)
-        normed = q_ref[:, cols].astype(F32) * conv_ref[:, cols] * scale * gain_ref[:, cols]
-        product = (km_ref[:, cols].astype(F32) * normed).astype(BF16)
-        out_ref[:, cols] = product
-        tail_ref[:, cols] = product[product.shape[0] - halo :]
+def spectrum_of(real, imag):
+    return jnp.concatenate([real.astype(BF16), imag.astype(BF16)], 0)
 
 
 def adjoint_kernel(width, nsq, *refs):
     sq = refs[:nsq]
     (up_ref, qm_ref, head_ref, f_ref, skip_ref, q_ref, conv_ref, km_ref, gain_ref,
-     fg_ref, fh_ref, inv_ref, gk_ref, gn_ref, w_ref) = refs[nsq:]
+     fg_ref, fh_ref, inv_ref, gk_ref, gn_ref, w_ref, z_ref, tail_ref, corr_ref,
+     scale_ref) = refs[nsq:]
     rows, block = q_ref.shape
+    taps = f_ref.shape[0]
     half = fg_ref.shape[0] // 2
 
     @pl.when(pl.program_id(0) == 0)
     def _():
         w_ref[...] = jnp.zeros_like(w_ref)
+        scale_ref[...] = jnp.broadcast_to(row_scale(width, *sq), scale_ref.shape)
 
     g = (up_ref[...].astype(F32) * qm_ref[...].astype(F32)).astype(BF16)
     gs = dot(fg_ref[...], jnp.concatenate([g, head_ref[...]], 0))
     hs = dot(fh_ref[...], f_ref[...].astype(BF16))
     hr, hi = hs[:half] + skip_ref[...], hs[half:]
     gr, gi = gs[:half], gs[half:]
-    spectrum = jnp.concatenate(
-        [(gr * hr + gi * hi).astype(BF16), (gi * hr - gr * hi).astype(BF16)], 0
-    )
-    gp = dot(inv_ref[:rows, :], spectrum)
-    scale = row_scale(width, *sq)
+    gp = dot(inv_ref[:rows, :], spectrum_of(gr * hr + gi * hi, gi * hr - gr * hi))
+    scale = scale_ref[...]
     for start in range(0, block, LANES):
         cols = slice(start, start + LANES)
         mixed = q_ref[:, cols].astype(F32) * conv_ref[:, cols]
         back = gp[:, cols]
         gain = gain_ref[:, cols]
-        gk_ref[:, cols] = (back * (mixed * scale * gain)).astype(BF16)
-        gn = back * km_ref[:, cols].astype(F32)
+        km = km_ref[:, cols].astype(F32)
+        normed = mixed * scale * gain
+        gk_ref[:, cols] = (back * normed).astype(BF16)
+        z_ref[:, cols] = (km * normed).astype(BF16)
+        gn = back * km
         gn_ref[:, cols] = gn
         w_ref[...] += gn * gain * mixed
-
-
-def medium_kernel(z_ref, tail_ref, up_ref, qm_ref, f_ref, skip_ref, fz_ref, fg_ref, fh_ref,
-                  inv_ref, gq_ref, corr_ref):
-    rows, block = up_ref.shape
-    half = fz_ref.shape[0] // 2
-    taps = f_ref.shape[0]
-    up = up_ref[...].astype(F32)
-    g = (up * qm_ref[...].astype(F32)).astype(BF16)
-    zs = dot(fz_ref[...], jnp.concatenate([tail_ref[...], z_ref[...]], 0))
-    hs = dot(fh_ref[...], f_ref[...].astype(BF16))
-    gs = dot(fg_ref[:, :rows], g)
-    hr, hi = hs[:half] + skip_ref[...], hs[half:]
+    tail_ref[...] = z_ref[rows - taps :, :]
+    zs = dot(fg_ref[:, :rows], z_ref[...])
     zr, zi = zs[:half], zs[half:]
-    gr, gi = gs[:half], gs[half:]
-    spectrum = jnp.concatenate(
-        [(zr * hr - zi * hi).astype(BF16), (zr * hi + zi * hr).astype(BF16)], 0
-    )
-    gq_ref[...] = (up * dot(inv_ref[:rows, :], spectrum)).astype(BF16)
-    cross = jnp.concatenate(
-        [(gr * zr + gi * zi).astype(BF16), (gi * zr - gr * zi).astype(BF16)], 0
-    )
-    corr = dot(inv_ref[:taps, :], cross)
+    corr = dot(inv_ref[:taps, :], spectrum_of(gr * zr + gi * zi, gi * zr - gr * zi))
     share = corr_ref.shape[2]
     for part in range(corr_ref.shape[0]):
         corr_ref[part] = corr[:, part * share : (part + 1) * share]
 
 
+def medium_kernel(z_ref, tail_ref, up_ref, f_ref, skip_ref, fz_ref, fh_ref, inv_ref, gq_ref):
+    rows, _ = up_ref.shape
+    half = fz_ref.shape[0] // 2
+    zs = dot(fz_ref[...], jnp.concatenate([tail_ref[...], z_ref[...]], 0))
+    hs = dot(fh_ref[...], f_ref[...].astype(BF16))
+    hr, hi = hs[:half] + skip_ref[...], hs[half:]
+    zr, zi = zs[:half], zs[half:]
+    conv = dot(inv_ref[:rows, :], spectrum_of(zr * hr - zi * hi, zr * hi + zi * hr))
+    gq_ref[...] = (up_ref[...].astype(F32) * conv).astype(BF16)
+
+
 def back_kernel(width, nsq, *refs):
     sq, ws = refs[:nsq], refs[nsq : 2 * nsq]
     (q_ref, k_ref, v_ref, tail_ref, head_ref, conv_ref, gn_ref, gain_ref, f_ref,
-     gq_ref, gk_ref, gv_ref, small_ref, pad_p, pad_g) = refs[2 * nsq :]
+     gq_ref, gk_ref, gv_ref, small_ref, pad_p, pad_g, scale_ref, coef_ref) = refs[2 * nsq :]
     rows, block = q_ref.shape
     halo = tail_ref.shape[0]
     taps = f_ref.shape[0]
     share = small_ref.shape[2]
-    scale = row_scale(width, *sq)
-    weight = ws[0][...]
-    for part in ws[1:]:
-        weight = weight + part[...]
-    coef = jnp.sum(weight, axis=1, keepdims=True) * (scale * scale * scale) * (1.0 / width)
+
+    @pl.when(pl.program_id(0) == 0)
+    def _():
+        scale = row_scale(width, *sq)
+        weight = ws[0][...]
+        for part in ws[1:]:
+            weight = weight + part[...]
+        coef = jnp.sum(weight, axis=1, keepdims=True) * (scale * scale * scale) * (1.0 / width)
+        scale_ref[...] = jnp.broadcast_to(scale, scale_ref.shape)
+        coef_ref[...] = jnp.broadcast_to(coef, coef_ref.shape)
+
+    scale, coef = scale_ref[...], coef_ref[...]
     for start in range(0, block, LANES):
         cols = slice(start, start + LANES)
         q = q_ref[:, cols].astype(F32)
@@ -250,11 +237,10 @@
     stream = rowed(rows)
     one = rowed(1)
 
-    def call(body, name, ins, specs, outs, out_specs, scratch=(), flops=0):
+    def call(body, ins, specs, outs, out_specs, scratch=(), flops=0):
         moved = sum(a.size * a.dtype.itemsize for a in list(ins) + list(outs))
         return pl.pallas_call(
             body,
-            name=name,
             grid=(steps,),
             in_specs=specs,
             out_specs=out_specs,
@@ -262,7 +248,7 @@
             scratch_shapes=scratch,
             cost_estimate=pl.CostEstimate(flops=flops, bytes_accessed=moved, transcendentals=0),
             compiler_params=pltpu.CompilerParams(
-                dimension_semantics=("arbitrary",), vmem_limit_bytes=56 * 2**20
+                dimension_semantics=("arbitrary",), vmem_limit_bytes=58 * 2**20
             ),
         )(*ins)
 
@@ -279,7 +265,7 @@
         (upstream[:taps].astype(F32) * query_mr[:taps].astype(F32)).astype(BF16), "ctx", -1
     )
     conv_se, squares = call(
-        short_kernel, "short",
+        short_kernel,
         (query_se, key_se, value_se, tail_se, filter_se),
         [stream, stream, stream, rowed(halo), rowed(taps_se)],
         [shape(rows, F32), lanes_shape], [stream, lanes_spec],
@@ -287,23 +273,21 @@
     )
     sq = exchanged(squares, "tp")
     nsq = len(sq)
-    product_mr, tail = call(
-        functools.partial(product_kernel, width, nsq), "product",
-        (*sq, query_se, conv_se, key_mr, gain),
-        [lanes_spec] * nsq + [stream, stream, stream, one],
-        [shape(rows, BF16), shape(taps, BF16)], [stream, rowed(taps)],
-    )
-    tail_mr = shifted(tail, "ctx", 1)
-    grad_key_mr, grad_normed, weight = call(
-        functools.partial(adjoint_kernel, width, nsq), "adjoint",
+    group_spec = pl.BlockSpec((block // group, taps, group), lambda i: (i, 0, 0))
+    grad_key_mr, grad_normed, weight, product_mr, tail, corr = call(
+        functools.partial(adjoint_kernel, width, nsq),
         (*sq, upstream, query_mr, head_mr, filter_mr, skip, query_se, conv_se, key_mr, gain,
          fg, fh, inv),
         [lanes_spec] * nsq
         + [stream, stream, rowed(taps), rowed(taps), one, stream, stream, stream, one,
            whole(fg), whole(fh), whole(inv)],
-        [shape(rows, BF16), shape(rows, F32), lanes_shape], [stream, stream, lanes_spec],
-        flops=2 * length * (length + taps + rows) * chans,
-    )
+        [shape(rows, BF16), shape(rows, F32), lanes_shape, shape(rows, BF16),
+         shape(taps, BF16), jax.ShapeDtypeStruct((chans // group, taps, group), F32)],
+        [stream, stream, lanes_spec, stream, rowed(taps), group_spec],
+        [pltpu.VMEM((rows, LANES), F32)],
+        flops=2 * length * (length + taps + 2 * rows + taps) * chans,
+    )
+    tail_mr = shifted(tail, "ctx", 1)
     ws = exchanged(weight, "tp")
     first = slice(0, halo)
     scale = lax.rsqrt(jnp.sum(sum(a[first] for a in sq), axis=1, keepdims=True) / width + EPSILON)
@@ -311,29 +295,28 @@
     q_head = query_se[first].astype(F32)
     mixed_head = gain * scale * grad_normed[first] - q_head * conv_se[first] * coef
     head_se = shifted((mixed_head * q_head).astype(BF16), "ctx", -1)
-    grad_query_mr, corr = call(
-        medium_kernel, "medium",
-        (product_mr, tail_mr, upstream, query_mr, filter_mr, skip, fz, fg, fh, inv),
-        [stream, rowed(taps), stream, stream, rowed(taps), one,
-         whole(fz), whole(fg), whole(fh), whole(inv)],
-        [shape(rows, BF16), jax.ShapeDtypeStruct((chans // group, taps, group), F32)],
-        [stream, pl.BlockSpec((block // group, taps, group), lambda i: (i, 0, 0))],
-        flops=2 * length * (length + taps + rows + rows + taps) * chans,
-    )
     grad_query_se, grad_key_se, grad_value_se, small = call(
-        functools.partial(back_kernel, width, nsq), "back",
+        functools.partial(back_kernel, width, nsq),
         (*sq, *ws, query_se, key_se, value_se, tail_se, head_se, conv_se, grad_normed, gain,
          filter_se),
         [lanes_spec] * (2 * nsq)
         + [stream, stream, stream, rowed(halo), rowed(halo), stream, stream, one, rowed(taps_se)],
         [shape(rows, BF16)] * 3 + [jax.ShapeDtypeStruct((chans // group, taps_se + 1, group), F32)],
         [stream] * 3 + [pl.BlockSpec((block // group, taps_se + 1, group), lambda i: (i, 0, 0))],
-        [pltpu.VMEM((halo + rows, LANES), F32), pltpu.VMEM((halo + rows, LANES), F32)],
+        [pltpu.VMEM((halo + rows, LANES), F32)] * 2 + [pltpu.VMEM((rows, LANES), F32)] * 2,
+    )
+    corr, small = split_parts(corr, share), split_parts(small, share)
+    small = lax.all_to_all(small, "ctx", 0, 0, tiled=True)
+    (grad_query_mr,) = call(
+        medium_kernel,
+        (product_mr, tail_mr, upstream, filter_mr, skip, fz, fh, inv),
+        [stream, rowed(taps), stream, rowed(taps), one, whole(fz), whole(fh), whole(inv)],
+        [shape(rows, BF16)], [stream],
+        flops=2 * length * (length + taps + rows) * chans,
     )
     factor = 1.0 / math.sqrt(tokens)
-    corr, small = split_parts(corr, share), split_parts(small, share)
     total_mr = scatter_sum(corr, "ctx") * factor
-    total = jnp.sum(lax.all_to_all(small, "ctx", 0, 0, tiled=True), axis=0) * factor
+    total = jnp.sum(small, axis=0) * factor
     return (
         grad_query_se,
         grad_key_se,
@@ -352,4 +335,5 @@
     in_specs = streams * 6 + (P(None, "tp"), P(None, "tp"), P("tp"), P("tp"))
     both = ("tp", "ctx")
     out_specs = streams * 5 + (P(None, both), P(None, both), P(both), P(both))
+
     return jax.shard_map(local, mesh=mesh, in_specs=in_specs, out_specs=out_specs, check_vma=False)

time: 138 us -> 114 us (0.83)
  starting transfers between devices: 50.6 us -> 37.3 us
  Pallas kernels: 53.1 us -> 45.1 us
  waiting for transfers between devices: 18.1 us -> 16.2 us
  local copies, waits for them, and re-layouts: 7.26 us -> 5.83 us
    ppermute x4, starting transfers between devices: 31 us -> 18.6 us  [scatter_sum(): got = lax.ppermute(away, axis, [(i, i ^ bit) for i in range(size)])]
    pallas_call x5 -> x4, Pallas kernels: 53.1 us -> 45.1 us  [call(): pl.pallas_call(body, grid=(steps,), in_specs=specs, out_specs=out_specs,...]
    ppermute x4, waiting for transfers between devices: 2.88 us -> 0.97 us  [shifted(): return lax.ppermute(block, axis, route)]
    unnamed x24 -> x18, local copies, waits for them, and re-layouts: 3.95 us -> 3.3 us
  transfers between devices with their start and end apart: 11 -> 11, of which waited for: 6 -> 5; matrix products, arithmetic and copies ran while one was open for 5% -> 5% of each run, Pallas kernels for 27% -> 19%
where the time goes in v1:
time: 114 us; the launch traced here: 113 us
  Pallas kernels  45.1 us (40%)
  starting transfers between devices  37.3 us (33%)
  waiting for transfers between devices  16.2 us (14%)
  other arithmetic  7.11 us (6%)
  local copies, waits for them, and re-layouts  5.83 us (5%)
    pallas_call x4, Pallas kernels, call(): pl.pallas_call(body, grid=(steps,), in_specs=specs, out_specs=out_specs,...  45.1 us
    ppermute x4, starting transfers between devices, scatter_sum(): got = lax.ppermute(away, axis, [(i, i ^ bit) for i in range(size)])  18.6 us
    ppermute x4, starting transfers between devices, shifted(): return lax.ppermute(block, axis, route)  8.72 us
    all_to_all x1, waiting for transfers between devices, local(): small = lax.all_to_all(small, 'ctx', 0, 0, tiled=True)  6.38 us
    ppermute x2, waiting for transfers between devices, exchanged(): lax.ppermute(value, axis, [(i, (i + step) % size) for i in range(size)])  5.98 us
    all_to_all x1, starting transfers between devices, local(): small = lax.all_to_all(small, 'ctx', 0, 0, tiled=True)  5.47 us
    ppermute x2, starting transfers between devices, exchanged(): lax.ppermute(value, axis, [(i, (i + step) % size) for i in range(size)])  4.47 us
    unnamed x18, local copies, waits for them, and re-layouts  3.3 us
  transfers between devices with their start and end apart: 11, of which 5 were waited for; matrix products, arithmetic and copies ran while one was open for 5% of the time, Pallas kernels for 19%

profile of v1, /device:TPU:0, one launch (start us, length us, event | category | flops | bytes accessed | tf_op | source)
XLA Modules:
  0.0 112.5 jit_solution(16343412906228494862)
XLA Ops:
  0.6 1.8 %multiply_convert_fusion = bf16[128,4096]{1,0:T(8,128)(2,1)S(1)} fusion(bf16[224,4096]{1,0:T(8,128)(2,1)} %refs_3_.1, bf16[224,4096]{1,0:T(8,128)(2,1)} %up_ref.1), kind=kLoop, calls=%fused_computation | loop fusion | flops 2097152 | bytes 3145728 | tf_op jit(solution)/shard_map/convert_element_type | solution.py:265
  2.4 1.3 %collective-permute-start.2 = (bf16[128,4096]{1,0:T(8,128)(2,1)S(1)}, bf16[128,4096]{1,0:T(8,128)(2,1)S(1)}, u32[]{:S(2)}, u32[]{:S(2)}) collective-permute-start(bf16[128,4096]{1,0:T(8,128)(2,1)S(1)} %multiply_convert_fusion), channel_id=1, source_target_pairs={{2,0},{4,2},{6,4},{8,6},{10,8},{12,10},{14,12},{16,14},{18,16},{20... | collective-permute-start | bytes 3145736 | tf_op jit(solution)/shard_map/ppermute | solution.py:22
  3.7 1.0 multiply_convert_fusion.1
  4.7 3.0 %collective-permute-start = (bf16[16,4096]{1,0:T(8,128)(2,1)S(1)}, bf16[16,4096]{1,0:T(8,128)(2,1)S(1)}, u32[]{:S(2)}, u32[]{:S(2)}) collective-permute-start(bf16[16,4096]{1,0:T(8,128)(2,1)S(1)} %multiply_convert_fusion.1), channel_id=1, source_target_pairs={{0,2},{2,4},{4,6},{6,8},{8,10},{10,12},{12,14},{14,16},{16,18},{18... | collective-permute-start | bytes 393224 | tf_op jit(solution)/shard_map/ppermute | solution.py:22
  9.4 8.6 %shard_map.205 = (f32[224,4096]{1,0:T(8,128)}, f32[224,128]{1,0:T(8,128)}) custom-call(bf16[224,4096]{1,0:T(8,128)(2,1)} %refs_4_.1, bf16[224,4096]{1,0:T(8,128)(2,1)} %refs_5_.3, bf16[224,4096]{1,0:T(8,128)(2,1)} %refs_6_.1, bf16[16,4096]{1,0:T(8,128)(2,1)} %copy-done.2, f32[7,4096]{1,0:T(8,128)} %refs_12_.2), custom_call_target="tpu_custom_call" | custom-call | bytes 9535488 | tf_op jit(solution)/shard_map/pallas_call | solution.py:242
  18.0 3.0 %collective-permute-start.1 = (f32[224,128]{1,0:T(8,128)}, f32[224,128]{1,0:T(8,128)S(1)}, u32[]{:S(2)}, u32[]{:S(2)}) collective-permute-start(f32[224,128]{1,0:T(8,128)} %get-tuple-element.21.refs_0_), channel_id=1, source_target_pairs={{0,1},{1,0},{2,3},{3,2},{4,5},{5,4},{6,7},{7,6},{8,9},{9,8},{10,11... | collective-permute-start | bytes 344072 | tf_op jit(solution)/shard_map/ppermute | solution.py:208
  20.9 3.0 %collective-permute-done.1.refs_1_ = f32[224,128]{1,0:T(8,128)S(1)} collective-permute-done((f32[224,128]{1,0:T(8,128)}, f32[224,128]{1,0:T(8,128)S(1)}, u32[]{:S(2)}, u32[]{:S(2)}) %collective-permute-start.1) | collective-permute-done | bytes 114720 | tf_op jit(solution)/shard_map/ppermute | solution.py:208
  24.9 13.9 %shard_map.206 = (bf16[224,4096]{1,0:T(8,128)(2,1)}, f32[224,4096]{1,0:T(8,128)}, f32[224,128]{1,0:T(8,128)}, bf16[224,4096]{1,0:T(8,128)(2,1)}, bf16[128,4096]{1,0:T(8,128)(2,1)}, /*index=5*/f32[16,128,256]{2,1,0:T(8,128)}) custom-call(f32[224,128]{1,0:T(8,128)} %get-tuple-element.21.refs_0_, f32[224,128]{1,0:T(8,128)} %copy-done.3, ...), custom_call_target="tpu_custom_call" | custom-call | flops 3045064704 | bytes 25513984 | tf_op jit(solution)/shard_map/pallas_call | solution.py:242
  38.9 1.3 %fusion = bf16[8,128,256]{2,1,0:T(8,128)(2,1)S(1)} fusion(f32[8,2,128,256]{3,2,1,0:T(8,128)} %bitcast.29, s32[]{:T(128)S(6)} %select_n.41), kind=kLoop, calls=%fused_computation.3 | loop fusion | bytes 1048580 | tf_op jit(solution)/shard_map/convert_element_type | solution.py:196
  40.2 10.7 %collective-permute-start.6 = (bf16[8,128,256]{2,1,0:T(8,128)(2,1)S(1)}, bf16[8,128,256]{2,1,0:T(8,128)(2,1)S(1)}, u32[]{:S(2)}, u32[]{:S(2)}) collective-permute-start(bf16[8,128,256]{2,1,0:T(8,128)(2,1)S(1)} %fusion), channel_id=1, source_target_pairs={{0,2},{2,0},{4,6},{6,4},{8,10},{10,8},{12,14},{14,12},{16,18},{18,... | collective-permute-start | bytes 1572872 | tf_op jit(solution)/shard_map/ppermute | solution.py:198
  50.9 1.5 %collective-permute-start.3 = (f32[224,128]{1,0:T(8,128)}, f32[224,128]{1,0:T(8,128)S(1)}, u32[]{:S(2)}, u32[]{:S(2)}) collective-permute-start(f32[224,128]{1,0:T(8,128)} %get-tuple-element.23.refs_2_), channel_id=1, source_target_pairs={{0,1},{1,0},{2,3},{3,2},{4,5},{5,4},{6,7},{7,6},{8,9},{9,8},{10,11... | collective-permute-start | bytes 344072 | tf_op jit(solution)/shard_map/ppermute | solution.py:208
  53.2 3.0 %collective-permute-done.3.refs_3_ = f32[224,128]{1,0:T(8,128)S(1)} collective-permute-done((f32[224,128]{1,0:T(8,128)}, f32[224,128]{1,0:T(8,128)S(1)}, u32[]{:S(2)}, u32[]{:S(2)}) %collective-permute-start.3) | collective-permute-done | bytes 114720 | tf_op jit(solution)/shard_map/ppermute | solution.py:208
  57.1 1.4 %bitcast_add_fusion = f32[8,128,256]{2,1,0:T(8,128)S(1)} fusion(bf16[8,128,256]{2,1,0:T(8,128)(2,1)S(1)} %collective-permute-done.6, f32[8,2,128,256]{3,2,1,0:T(8,128)} %bitcast.30, s32[]{:T(128)S(6)} %select_n.40), kind=kLoop, calls=%fused_computation.2 | loop fusion | flops 524288 | bytes 2621444 | tf_op jit(solution)/shard_map/add | solution.py:199
  58.5 4.0 %collective-permute-start.7 = (bf16[4,128,256]{2,1,0:T(8,128)(2,1)S(1)}, bf16[4,128,256]{2,1,0:T(8,128)(2,1)S(1)}, u32[]{:S(2)}, u32[]{:S(2)}) collective-permute-start(bf16[4,128,256]{2,1,0:T(8,128)(2,1)S(1)} %fusion.4), channel_id=1, source_target_pairs={{0,4},{2,6},{4,0},{6,2},{8,12},{10,14},{12,8},{14,10},{16,20},{18,... | collective-permute-start | bytes 786440 | tf_op jit(solution)/shard_map/ppermute | solution.py:198
  62.5 1.2 %fusion.3 = bf16[16,4096]{1,0:T(8,128)(2,1)S(1)} fusion(f32[224,4096]{1,0:T(8,128)} %get-tuple-element.22.refs_8_.refs_9_, f32[224,4096]{1,0:T(8,128)} %get-tuple-element.24.refs_10_, f32[16]{0:T(128)S(1)} %get-tuple-element.34, bf16[224,4096]{1,0:T(8,128)(2,1)} %refs_4_.1, f32[16]{0:T(128)S(1)} %get-tuple-element.33, f32[4096]{0:T(1024)S(1)} %copy-done.4), kind=kLoop, calls=%fused_computation.10 | loop fusion | flops 524288 | bytes 802944 | tf_op jit(solution)/shard_map/convert_element_type | solution.py:297
  63.7 1.3 %collective-permute-start.4 = (bf16[16,4096]{1,0:T(8,128)(2,1)S(1)}, bf16[16,4096]{1,0:T(8,128)(2,1)S(1)}, u32[]{:S(2)}, u32[]{:S(2)}) collective-permute-start(bf16[16,4096]{1,0:T(8,128)(2,1)S(1)} %fusion.3), channel_id=1, source_target_pairs={{2,0},{4,2},{6,4},{8,6},{10,8},{12,10},{14,12},{16,14},{18,16},{20... | collective-permute-start | bytes 393224 | tf_op jit(solution)/shard_map/ppermute | solution.py:22
  65.0 3.1 %collective-permute-start.5 = (bf16[128,4096]{1,0:T(8,128)(2,1)}, bf16[128,4096]{1,0:T(8,128)(2,1)S(1)}, u32[]{:S(2)}, u32[]{:S(2)}) collective-permute-start(bf16[128,4096]{1,0:T(8,128)(2,1)} %get-tuple-element.29), channel_id=1, source_target_pairs={{0,2},{2,4},{4,6},{6,8},{8,10},{10,12},{12,14},{14,16},{16,18},{18... | collective-permute-start | bytes 3145736 | tf_op jit(solution)/shard_map/ppermute | solution.py:22
  68.8 12.8 %shard_map.207 = (bf16[224,4096]{1,0:T(8,128)(2,1)}, bf16[224,4096]{1,0:T(8,128)(2,1)}, bf16[224,4096]{1,0:T(8,128)(2,1)}, f32[16,8,256]{2,1,0:T(8,128)}) custom-call(f32[224,128]{1,0:T(8,128)} %get-tuple-element.21.refs_0_, f32[224,128]{1,0:T(8,128)} %copy-done.3, f32[224,128]{1,0:T(8,128)} %get-tuple-element.23.refs_2_, f32[224,128]{1,0:T(8,128)} %copy-done.6, ...), custom_call_target="tpu_custom_call" | custom-call | bytes 19333120 | tf_op jit(solution)/shard_map/pallas_call | solution.py:242
  81.6 5.5 %all-to-all-start = ((f32[16,8,256]{2,1,0:T(8,128)}), f32[16,8,256]{2,1,0:T(8,128)S(1)}, u32[]{:S(2)}, u32[]{:S(2)}) async-start(f32[16,8,256]{2,1,0:T(8,128)} %get-tuple-element.31), calls=%async_computation | async-start | bytes 262144 | tf_op jit(solution)/shard_map/all_to_all | solution.py:309
  87.2 2.0 %collective-permute-start.8 = (bf16[2,128,256]{2,1,0:T(8,128)(2,1)S(1)}, bf16[2,128,256]{2,1,0:T(8,128)(2,1)S(1)}, u32[]{:S(2)}, u32[]{:S(2)}) collective-permute-start(bf16[2,128,256]{2,1,0:T(8,128)(2,1)S(1)} %fusion.5), channel_id=1, source_target_pairs={{0,8},{2,10},{4,12},{6,14},{8,0},{10,2},{12,4},{14,6},{16,24},{18,... | collective-permute-start | bytes 393224 | tf_op jit(solution)/shard_map/ppermute | solution.py:198
  89.2 6.4 %all-to-all-done = f32[16,8,256]{2,1,0:T(8,128)S(1)} async-done(((f32[16,8,256]{2,1,0:T(8,128)}), f32[16,8,256]{2,1,0:T(8,128)S(1)}, u32[]{:S(2)}, u32[]{:S(2)}) %all-to-all-start) | async-done | bytes 131104 | tf_op jit(solution)/shard_map/all_to_all | solution.py:309
  95.7 1.9 %collective-permute-start.9 = (bf16[1,128,256]{2,1,0:T(8,128)(2,1)S(1)}, bf16[1,128,256]{2,1,0:T(8,128)(2,1)S(1)}, u32[]{:S(2)}, u32[]{:S(2)}) collective-permute-start(bf16[1,128,256]{2,1,0:T(8,128)(2,1)S(1)} %dynamic-slice_convert_fusion.2), channel_id=1, source_target_pairs={{0,16},{2,18},{4,20},{6,22},{8,24},{10,26},{12,28},{14,30},{16,0},... | collective-permute-start | bytes 196616 | tf_op jit(solution)/shard_map/ppermute | solution.py:198
  98.2 2.9 %collective-permute-done.9 = bf16[1,128,256]{2,1,0:T(8,128)(2,1)S(1)} collective-permute-done((bf16[1,128,256]{2,1,0:T(8,128)(2,1)S(1)}, bf16[1,128,256]{2,1,0:T(8,128)(2,1)S(1)}, u32[]{:S(2)}, u32[]{:S(2)}) %collective-permute-start.9) | collective-permute-done | bytes 65568 | tf_op jit(solution)/shard_map/ppermute | solution.py:198
  102.7 9.8 %shard_map.208 = bf16[224,4096]{1,0:T(8,128)(2,1)} custom-call(bf16[224,4096]{1,0:T(8,128)(2,1)} %get-tuple-element.28.z_ref, bf16[128,4096]{1,0:T(8,128)(2,1)} %copy-done.1, bf16[224,4096]{1,0:T(8,128)(2,1)} %up_ref.1, f32[128,4096]{1,0:T(8,128)} %f_ref.3, f32[1,4096]{1,0:T(1,128)} %bitcast.35, bf16[352,352]{1,0:T(8,128)(2,1)} %constant.105.clone.fz_ref, ...), custom_call_target="tpu_custom_call" | custom-call | flops 2030043136 | bytes 9162752 | tf_op jit(solution)/shard_map/pallas_call | solution.py:242
  (38 shorter events, 7.3 us)
Async XLA Ops:
  2.4 21.5 %collective-permute-start.2 = (bf16[128,4096]{1,0:T(8,128)(2,1)S(1)}, bf16[128,4096]{1,0:T(8,128)(2,1)S(1)}, u32[]{:S(2)}, u32[]{:S(2)}) collective-permute-start(bf16[128,4096]{1,0:T(8,128)(2,1)S(1)} %multiply_convert_fusion), channel_id=1, source_target_pairs={{2,0},{4,2},{6,4},{8,6},{10,8},{12,10},{14,12},{16,14},{18,16},{20... | collective-permute-start | bytes 3145736 | tf_op jit(solution)/shard_map/ppermute | solution.py:22
  4.7 4.0 %collective-permute-start = (bf16[16,4096]{1,0:T(8,128)(2,1)S(1)}, bf16[16,4096]{1,0:T(8,128)(2,1)S(1)}, u32[]{:S(2)}, u32[]{:S(2)}) collective-permute-start(bf16[16,4096]{1,0:T(8,128)(2,1)S(1)} %multiply_convert_fusion.1), channel_id=1, source_target_pairs={{0,2},{2,4},{4,6},{6,8},{8,10},{10,12},{12,14},{14,16},{16,18},{18... | collective-permute-start | bytes 393224 | tf_op jit(solution)/shard_map/ppermute | solution.py:22
  8.8 0.7 copy-start.2
  18.0 5.9 %collective-permute-start.1 = (f32[224,128]{1,0:T(8,128)}, f32[224,128]{1,0:T(8,128)S(1)}, u32[]{:S(2)}, u32[]{:S(2)}) collective-permute-start(f32[224,128]{1,0:T(8,128)} %get-tuple-element.21.refs_0_), channel_id=1, source_target_pairs={{0,1},{1,0},{2,3},{3,2},{4,5},{5,4},{6,7},{7,6},{8,9},{9,8},{10,11... | collective-permute-start | bytes 344072 | tf_op jit(solution)/shard_map/ppermute | solution.py:208
  23.9 0.6 copy-start.3
  23.9 1.0 copy-start
  40.2 22.3 %copy-start.4 = (f32[4096]{0:T(1024)S(1)}, f32[4096]{0:T(1024)}, u32[]{:S(2)}) copy-start(f32[4096]{0:T(1024)} %param.23) | copy-start | bytes 49156
  40.2 16.9 %collective-permute-start.6 = (bf16[8,128,256]{2,1,0:T(8,128)(2,1)S(1)}, bf16[8,128,256]{2,1,0:T(8,128)(2,1)S(1)}, u32[]{:S(2)}, u32[]{:S(2)}) collective-permute-start(bf16[8,128,256]{2,1,0:T(8,128)(2,1)S(1)} %fusion), channel_id=1, source_target_pairs={{0,2},{2,0},{4,6},{6,4},{8,10},{10,8},{12,14},{14,12},{16,18},{18,... | collective-permute-start | bytes 1572872 | tf_op jit(solution)/shard_map/ppermute | solution.py:198
  50.9 5.3 %collective-permute-start.3 = (f32[224,128]{1,0:T(8,128)}, f32[224,128]{1,0:T(8,128)S(1)}, u32[]{:S(2)}, u32[]{:S(2)}) collective-permute-start(f32[224,128]{1,0:T(8,128)} %get-tuple-element.23.refs_2_), channel_id=1, source_target_pairs={{0,1},{1,0},{2,3},{3,2},{4,5},{5,4},{6,7},{7,6},{8,9},{9,8},{10,11... | collective-permute-start | bytes 344072 | tf_op jit(solution)/shard_map/ppermute | solution.py:208
  56.2 7.4 %copy-start.6 = (f32[224,128]{1,0:T(8,128)}, f32[224,128]{1,0:T(8,128)S(1)}, u32[]{:S(2)}) copy-start(f32[224,128]{1,0:T(8,128)S(1)} %collective-permute-done.3.refs_3_) | copy-start | bytes 344068
  58.5 28.6 %collective-permute-start.7 = (bf16[4,128,256]{2,1,0:T(8,128)(2,1)S(1)}, bf16[4,128,256]{2,1,0:T(8,128)(2,1)S(1)}, u32[]{:S(2)}, u32[]{:S(2)}) collective-permute-start(bf16[4,128,256]{2,1,0:T(8,128)(2,1)S(1)} %fusion.4), channel_id=1, source_target_pairs={{0,4},{2,6},{4,0},{6,2},{8,12},{10,14},{12,8},{14,10},{16,20},{18,... | collective-permute-start | bytes 786440 | tf_op jit(solution)/shard_map/ppermute | solution.py:198
  63.7 4.4 %collective-permute-start.4 = (bf16[16,4096]{1,0:T(8,128)(2,1)S(1)}, bf16[16,4096]{1,0:T(8,128)(2,1)S(1)}, u32[]{:S(2)}, u32[]{:S(2)}) collective-permute-start(bf16[16,4096]{1,0:T(8,128)(2,1)S(1)} %fusion.3), channel_id=1, source_target_pairs={{2,0},{4,2},{6,4},{8,6},{10,8},{12,10},{14,12},{16,14},{18,16},{20... | collective-permute-start | bytes 393224 | tf_op jit(solution)/shard_map/ppermute | solution.py:22
  65.0 36.7 %collective-permute-start.5 = (bf16[128,4096]{1,0:T(8,128)(2,1)}, bf16[128,4096]{1,0:T(8,128)(2,1)S(1)}, u32[]{:S(2)}, u32[]{:S(2)}) collective-permute-start(bf16[128,4096]{1,0:T(8,128)(2,1)} %get-tuple-element.29), channel_id=1, source_target_pairs={{0,2},{2,4},{4,6},{6,8},{8,10},{10,12},{12,14},{14,16},{16,18},{18... | collective-permute-start | bytes 3145736 | tf_op jit(solution)/shard_map/ppermute | solution.py:22
  68.1 0.7 copy-start.7
  81.6 14.0 %all-to-all-start = ((f32[16,8,256]{2,1,0:T(8,128)}), f32[16,8,256]{2,1,0:T(8,128)S(1)}, u32[]{:S(2)}, u32[]{:S(2)}) async-start(f32[16,8,256]{2,1,0:T(8,128)} %get-tuple-element.31), calls=%async_computation | async-start | bytes 262144 | tf_op jit(solution)/shard_map/all_to_all | solution.py:309
  87.2 8.4 %collective-permute-start.8 = (bf16[2,128,256]{2,1,0:T(8,128)(2,1)S(1)}, bf16[2,128,256]{2,1,0:T(8,128)(2,1)S(1)}, u32[]{:S(2)}, u32[]{:S(2)}) collective-permute-start(bf16[2,128,256]{2,1,0:T(8,128)(2,1)S(1)} %fusion.5), channel_id=1, source_target_pairs={{0,8},{2,10},{4,12},{6,14},{8,0},{10,2},{12,4},{14,6},{16,24},{18,... | collective-permute-start | bytes 393224 | tf_op jit(solution)/shard_map/ppermute | solution.py:198
  95.7 5.4 %collective-permute-start.9 = (bf16[1,128,256]{2,1,0:T(8,128)(2,1)S(1)}, bf16[1,128,256]{2,1,0:T(8,128)(2,1)S(1)}, u32[]{:S(2)}, u32[]{:S(2)}) collective-permute-start(bf16[1,128,256]{2,1,0:T(8,128)(2,1)S(1)} %dynamic-slice_convert_fusion.2), channel_id=1, source_target_pairs={{0,16},{2,18},{4,20},{6,22},{8,24},{10,26},{12,28},{14,30},{16,0},... | collective-permute-start | bytes 196616 | tf_op jit(solution)/shard_map/ppermute | solution.py:198
  97.6 14.9 %copy-start.8 = (f32[8,256]{1,0:T(8,128)}, f32[8,256]{1,0:T(8,128)S(1)}, u32[]{:S(2)}) copy-start(f32[8,256]{1,0:T(8,128)S(1)} %broadcast_multiply_fusion) | copy-start | bytes 24580
  101.1 11.4 %copy-start.5 = (f32[1,128,256]{2,1,0:T(8,128)}, f32[1,128,256]{2,1,0:T(8,128)S(1)}, u32[]{:S(2)}) copy-start(f32[1,128,256]{2,1,0:T(8,128)S(1)} %add_multiply_fusion) | copy-start | bytes 393220
  101.7 1.0 copy-start.1

commit v2 on v1

--- a/solution.py
+++ b/solution.py
@@ -126,9 +126,9 @@
 
 
 def back_kernel(width, nsq, *refs):
-    sq, ws = refs[:nsq], refs[nsq : 2 * nsq]
+    scale_ref, ws = refs[0], refs[1 : 1 + nsq]
     (q_ref, k_ref, v_ref, tail_ref, head_ref, conv_ref, gn_ref, gain_ref, f_ref,
-     gq_ref, gk_ref, gv_ref, small_ref, pad_p, pad_g, scale_ref, coef_ref) = refs[2 * nsq :]
+     gq_ref, gk_ref, gv_ref, small_ref, pad_p, pad_g, coef_ref) = refs[1 + nsq :]
     rows, block = q_ref.shape
     halo = tail_ref.shape[0]
     taps = f_ref.shape[0]
@@ -136,13 +136,12 @@
 
     @pl.when(pl.program_id(0) == 0)
     def _():
-        scale = row_scale(width, *sq)
+        scale = scale_ref[...]
         weight = ws[0][...]
         for part in ws[1:]:
             weight = weight + part[...]
         coef = jnp.sum(weight, axis=1, keepdims=True) * (scale * scale * scale) * (1.0 / width)
-        scale_ref[...] = jnp.broadcast_to(scale, scale_ref.shape)
-        coef_ref[...] = jnp.broadcast_to(coef, coef_ref.shape)
+        coef_ref[...] = coef
 
     scale, coef = scale_ref[...], coef_ref[...]
     for start in range(0, block, LANES):
@@ -274,7 +273,7 @@
     sq = exchanged(squares, "tp")
     nsq = len(sq)
     group_spec = pl.BlockSpec((block // group, taps, group), lambda i: (i, 0, 0))
-    grad_key_mr, grad_normed, weight, product_mr, tail, corr = call(
+    grad_key_mr, grad_normed, weight, product_mr, tail, corr, scales = call(
         functools.partial(adjoint_kernel, width, nsq),
         (*sq, upstream, query_mr, head_mr, filter_mr, skip, query_se, conv_se, key_mr, gain,
          fg, fh, inv),
@@ -282,28 +281,29 @@
         + [stream, stream, rowed(taps), rowed(taps), one, stream, stream, stream, one,
            whole(fg), whole(fh), whole(inv)],
         [shape(rows, BF16), shape(rows, F32), lanes_shape, shape(rows, BF16),
-         shape(taps, BF16), jax.ShapeDtypeStruct((chans // group, taps, group), F32)],
-        [stream, stream, lanes_spec, stream, rowed(taps), group_spec],
-        [pltpu.VMEM((rows, LANES), F32)],
+         shape(taps, BF16), jax.ShapeDtypeStruct((chans // group, taps, group), F32),
+         lanes_shape],
+        [stream, stream, lanes_spec, stream, rowed(taps), group_spec, lanes_spec],
         flops=2 * length * (length + taps + 2 * rows + taps) * chans,
     )
     tail_mr = shifted(tail, "ctx", 1)
     ws = exchanged(weight, "tp")
     first = slice(0, halo)
-    scale = lax.rsqrt(jnp.sum(sum(a[first] for a in sq), axis=1, keepdims=True) / width + EPSILON)
+    scale = scales[first, :1]
     coef = scale**3 * jnp.sum(sum(a[first] for a in ws), axis=1, keepdims=True) / width
     q_head = query_se[first].astype(F32)
     mixed_head = gain * scale * grad_normed[first] - q_head * conv_se[first] * coef
-    head_se = shifted((mixed_head * q_head).astype(BF16), "ctx", -1)
+    head_send = (mixed_head * q_head).astype(BF16)
+    head_se = shifted(head_send, "ctx", -1)
     grad_query_se, grad_key_se, grad_value_se, small = call(
         functools.partial(back_kernel, width, nsq),
-        (*sq, *ws, query_se, key_se, value_se, tail_se, head_se, conv_se, grad_normed, gain,
+        (scales, *ws, query_se, key_se, value_se, tail_se, head_se, conv_se, grad_normed, gain,
          filter_se),
-        [lanes_spec] * (2 * nsq)
+        [lanes_spec] * (1 + nsq)
         + [stream, stream, stream, rowed(halo), rowed(halo), stream, stream, one, rowed(taps_se)],
         [shape(rows, BF16)] * 3 + [jax.ShapeDtypeStruct((chans // group, taps_se + 1, group), F32)],
         [stream] * 3 + [pl.BlockSpec((block // group, taps_se + 1, group), lambda i: (i, 0, 0))],
-        [pltpu.VMEM((halo + rows, LANES), F32)] * 2 + [pltpu.VMEM((rows, LANES), F32)] * 2,
+        [pltpu.VMEM((halo + rows, LANES), F32)] * 2 + [pltpu.VMEM((rows, LANES), F32)],
     )
     corr, small = split_parts(corr, share), split_parts(small, share)
     small = lax.all_to_all(small, "ctx", 0, 0, tiled=True)

time: 114 us -> 115 us (level)
  no operation moved by 1% of the time
where the time goes in v2:
time: 115 us; the launch traced here: 113 us
  Pallas kernels  45 us (39%)
  starting transfers between devices  37.3 us (32%)
  waiting for transfers between devices  17.1 us (15%)
  other arithmetic  7.08 us (6%)
  local copies, waits for them, and re-layouts  5.92 us (5%)
    pallas_call x4, Pallas kernels, call(): pl.pallas_call(body, grid=(steps,), in_specs=specs, out_specs=out_specs,...  45 us
    ppermute x4, starting transfers between devices, scatter_sum(): got = lax.ppermute(away, axis, [(i, i ^ bit) for i in range(size)])  18.6 us
    ppermute x4, starting transfers between devices, shifted(): return lax.ppermute(block, axis, route)  8.72 us
    ppermute x2, waiting for transfers between devices, exchanged(): lax.ppermute(value, axis, [(i, (i + step) % size) for i in range(size)])  6.82 us
    all_to_all x1, waiting for transfers between devices, local(): small = lax.all_to_all(small, 'ctx', 0, 0, tiled=True)  6.38 us
    all_to_all x1, starting transfers between devices, local(): small = lax.all_to_all(small, 'ctx', 0, 0, tiled=True)  5.46 us
    ppermute x2, starting transfers between devices, exchanged(): lax.ppermute(value, axis, [(i, (i + step) % size) for i in range(size)])  4.46 us
    unnamed x18, local copies, waits for them, and re-layouts  3.3 us
  transfers between devices with their start and end apart: 11, of which 5 were waited for; matrix products, arithmetic and copies ran while one was open for 5% of the time, Pallas kernels for 19%

profile of v2, /device:TPU:0, one launch (start us, length us, event | category | flops | bytes accessed | tf_op | source)
XLA Modules:
  0.0 113.3 jit_solution(16159399020085002852)
XLA Ops:
  0.6 1.8 %multiply_convert_fusion = bf16[128,4096]{1,0:T(8,128)(2,1)S(1)} fusion(bf16[224,4096]{1,0:T(8,128)(2,1)} %refs_3_.2, bf16[224,4096]{1,0:T(8,128)(2,1)} %up_ref.1), kind=kLoop, calls=%fused_computation | loop fusion | flops 2097152 | bytes 3145728 | tf_op jit(solution)/shard_map/convert_element_type | solution.py:264
  2.4 1.3 %collective-permute-start.2 = (bf16[128,4096]{1,0:T(8,128)(2,1)S(1)}, bf16[128,4096]{1,0:T(8,128)(2,1)S(1)}, u32[]{:S(2)}, u32[]{:S(2)}) collective-permute-start(bf16[128,4096]{1,0:T(8,128)(2,1)S(1)} %multiply_convert_fusion), channel_id=1, source_target_pairs={{2,0},{4,2},{6,4},{8,6},{10,8},{12,10},{14,12},{16,14},{18,16},{20... | collective-permute-start | bytes 3145736 | tf_op jit(solution)/shard_map/ppermute | solution.py:22
  3.7 1.0 multiply_convert_fusion.1
  4.7 3.0 %collective-permute-start = (bf16[16,4096]{1,0:T(8,128)(2,1)S(1)}, bf16[16,4096]{1,0:T(8,128)(2,1)S(1)}, u32[]{:S(2)}, u32[]{:S(2)}) collective-permute-start(bf16[16,4096]{1,0:T(8,128)(2,1)S(1)} %multiply_convert_fusion.1), channel_id=1, source_target_pairs={{0,2},{2,4},{4,6},{6,8},{8,10},{10,12},{12,14},{14,16},{16,18},{18... | collective-permute-start | bytes 393224 | tf_op jit(solution)/shard_map/ppermute | solution.py:22
  9.4 8.5 %shard_map.205 = (f32[224,4096]{1,0:T(8,128)}, f32[224,128]{1,0:T(8,128)}) custom-call(bf16[224,4096]{1,0:T(8,128)(2,1)} %refs_3_.3, bf16[224,4096]{1,0:T(8,128)(2,1)} %refs_4_.1, bf16[224,4096]{1,0:T(8,128)(2,1)} %refs_5_.3, bf16[16,4096]{1,0:T(8,128)(2,1)} %copy-done.2, f32[7,4096]{1,0:T(8,128)} %refs_11_.2), custom_call_target="tpu_custom_call" | custom-call | bytes 9535488 | tf_op jit(solution)/shard_map/pallas_call | solution.py:241
  17.9 3.0 %collective-permute-start.1 = (f32[224,128]{1,0:T(8,128)}, f32[224,128]{1,0:T(8,128)S(1)}, u32[]{:S(2)}, u32[]{:S(2)}) collective-permute-start(f32[224,128]{1,0:T(8,128)} %get-tuple-element.22.refs_0_), channel_id=1, source_target_pairs={{0,1},{1,0},{2,3},{3,2},{4,5},{5,4},{6,7},{7,6},{8,9},{9,8},{10,11... | collective-permute-start | bytes 344072 | tf_op jit(solution)/shard_map/ppermute | solution.py:207
  20.9 3.0 %collective-permute-done.1.refs_1_ = f32[224,128]{1,0:T(8,128)S(1)} collective-permute-done((f32[224,128]{1,0:T(8,128)}, f32[224,128]{1,0:T(8,128)S(1)}, u32[]{:S(2)}, u32[]{:S(2)}) %collective-permute-start.1) | collective-permute-done | bytes 114720 | tf_op jit(solution)/shard_map/ppermute | solution.py:207
  24.9 14.0 %shard_map.206 = (bf16[224,4096]{1,0:T(8,128)(2,1)}, f32[224,4096]{1,0:T(8,128)}, f32[224,128]{1,0:T(8,128)}, bf16[224,4096]{1,0:T(8,128)(2,1)}, bf16[128,4096]{...) custom-call(f32[224,128]{1,0:T(8,128)} %get-tuple-element.22.refs_0_, f32[224,128]{1,0:T(8,128)} %copy-done.7, ...), custom_call_target="tpu_custom_call" | custom-call | flops 3045064704 | bytes 25628672 | tf_op jit(solution)/shard_map/pallas_call | solution.py:241
  38.9 1.3 %fusion = bf16[8,128,256]{2,1,0:T(8,128)(2,1)S(1)} fusion(f32[8,2,128,256]{3,2,1,0:T(8,128)} %bitcast.30, s32[]{:T(128)S(6)} %select_n.41), kind=kLoop, calls=%fused_computation.3 | loop fusion | bytes 1048580 | tf_op jit(solution)/shard_map/convert_element_type | solution.py:195
  40.2 10.7 %collective-permute-start.6 = (bf16[8,128,256]{2,1,0:T(8,128)(2,1)S(1)}, bf16[8,128,256]{2,1,0:T(8,128)(2,1)S(1)}, u32[]{:S(2)}, u32[]{:S(2)}) collective-permute-start(bf16[8,128,256]{2,1,0:T(8,128)(2,1)S(1)} %fusion), channel_id=1, source_target_pairs={{0,2},{2,0},{4,6},{6,4},{8,10},{10,8},{12,14},{14,12},{16,18},{18,... | collective-permute-start | bytes 1572872 | tf_op jit(solution)/shard_map/ppermute | solution.py:197
  50.9 1.5 %collective-permute-start.3 = (f32[224,128]{1,0:T(8,128)}, f32[224,128]{1,0:T(8,128)S(1)}, u32[]{:S(2)}, u32[]{:S(2)}) collective-permute-start(f32[224,128]{1,0:T(8,128)} %get-tuple-element.25.refs_1_), channel_id=1, source_target_pairs={{0,1},{1,0},{2,3},{3,2},{4,5},{5,4},{6,7},{7,6},{8,9},{9,8},{10,11... | collective-permute-start | bytes 344072 | tf_op jit(solution)/shard_map/ppermute | solution.py:207
  52.4 3.8 %collective-permute-done.3.refs_2_ = f32[224,128]{1,0:T(8,128)S(1)} collective-permute-done((f32[224,128]{1,0:T(8,128)}, f32[224,128]{1,0:T(8,128)S(1)}, u32[]{:S(2)}, u32[]{:S(2)}) %collective-permute-start.3) | collective-permute-done | bytes 114720 | tf_op jit(solution)/shard_map/ppermute | solution.py:207
  57.9 1.4 %bitcast_add_fusion = f32[8,128,256]{2,1,0:T(8,128)S(1)} fusion(bf16[8,128,256]{2,1,0:T(8,128)(2,1)S(1)} %collective-permute-done.6, f32[8,2,128,256]{3,2,1,0:T(8,128)} %bitcast.31, s32[]{:T(128)S(6)} %select_n.40), kind=kLoop, calls=%fused_computation.2 | loop fusion | flops 524288 | bytes 2621444 | tf_op jit(solution)/shard_map/add | solution.py:198
  59.4 4.0 %collective-permute-start.7 = (bf16[4,128,256]{2,1,0:T(8,128)(2,1)S(1)}, bf16[4,128,256]{2,1,0:T(8,128)(2,1)S(1)}, u32[]{:S(2)}, u32[]{:S(2)}) collective-permute-start(bf16[4,128,256]{2,1,0:T(8,128)(2,1)S(1)} %fusion.4), channel_id=1, source_target_pairs={{0,4},{2,6},{4,0},{6,2},{8,12},{10,14},{12,8},{14,10},{16,20},{18,... | collective-permute-start | bytes 786440 | tf_op jit(solution)/shard_map/ppermute | solution.py:197
  63.4 1.2 %fusion.3 = bf16[16,4096]{1,0:T(8,128)(2,1)S(1)} fusion(f32[224,4096]{1,0:T(8,128)} %get-tuple-element.23.refs_8_, f32[224,4096]{1,0:T(8,128)} %get-tuple-element.26.refs_9_, f32[16]{0:T(128)S(1)} %get-tuple-element.36, bf16[224,4096]{1,0:T(8,128)(2,1)} %refs_3_.3, f32[16]{0:T(128)S(1)} %get-tuple-element.35, f32[4096]{0:T(1024)S(1)} %copy-done.3), kind=kLoop, calls=%fused_computation.10 | loop fusion | flops 524288 | bytes 802944 | tf_op jit(solution)/shard_map/convert_element_type | solution.py:296
  64.6 1.3 %collective-permute-start.4 = (bf16[16,4096]{1,0:T(8,128)(2,1)S(1)}, bf16[16,4096]{1,0:T(8,128)(2,1)S(1)}, u32[]{:S(2)}, u32[]{:S(2)}) collective-permute-start(bf16[16,4096]{1,0:T(8,128)(2,1)S(1)} %fusion.3), channel_id=1, source_target_pairs={{2,0},{4,2},{6,4},{8,6},{10,8},{12,10},{14,12},{16,14},{18,16},{20... | collective-permute-start | bytes 393224 | tf_op jit(solution)/shard_map/ppermute | solution.py:22
  65.9 3.1 %collective-permute-start.5 = (bf16[128,4096]{1,0:T(8,128)(2,1)}, bf16[128,4096]{1,0:T(8,128)(2,1)S(1)}, u32[]{:S(2)}, u32[]{:S(2)}) collective-permute-start(bf16[128,4096]{1,0:T(8,128)(2,1)} %get-tuple-element.31), channel_id=1, source_target_pairs={{0,2},{2,4},{4,6},{6,8},{8,10},{10,12},{12,14},{14,16},{16,18},{18... | collective-permute-start | bytes 3145736 | tf_op jit(solution)/shard_map/ppermute | solution.py:22
  69.7 12.7 %shard_map.207 = (bf16[224,4096]{1,0:T(8,128)(2,1)}, bf16[224,4096]{1,0:T(8,128)(2,1)}, bf16[224,4096]{1,0:T(8,128)(2,1)}, f32[16,8,256]{2,1,0:T(8,128)}) custom-call(f32[224,128]{1,0:T(8,128)} %get-tuple-element.24.refs_0_, f32[224,128]{1,0:T(8,128)} %get-tuple-element.25.refs_1_, f32[224,128]{1,0:T(8,128)} %copy-done.5, bf16[224,4096]{1,0:T(8,128)(2,1)} %refs_3_.3, ...), custom_call_target="tpu_custom_call" | custom-call | bytes 19218432 | tf_op jit(solution)/shard_map/pallas_call | solution.py:241
  82.4 5.5 %all-to-all-start = ((f32[16,8,256]{2,1,0:T(8,128)}), f32[16,8,256]{2,1,0:T(8,128)S(1)}, u32[]{:S(2)}, u32[]{:S(2)}) async-start(f32[16,8,256]{2,1,0:T(8,128)} %get-tuple-element.33), calls=%async_computation | async-start | bytes 262144 | tf_op jit(solution)/shard_map/all_to_all | solution.py:309
  88.0 2.0 %collective-permute-start.8 = (bf16[2,128,256]{2,1,0:T(8,128)(2,1)S(1)}, bf16[2,128,256]{2,1,0:T(8,128)(2,1)S(1)}, u32[]{:S(2)}, u32[]{:S(2)}) collective-permute-start(bf16[2,128,256]{2,1,0:T(8,128)(2,1)S(1)} %fusion.5), channel_id=1, source_target_pairs={{0,8},{2,10},{4,12},{6,14},{8,0},{10,2},{12,4},{14,6},{16,24},{18,... | collective-permute-start | bytes 393224 | tf_op jit(solution)/shard_map/ppermute | solution.py:197
  90.0 6.4 %all-to-all-done = f32[16,8,256]{2,1,0:T(8,128)S(1)} async-done(((f32[16,8,256]{2,1,0:T(8,128)}), f32[16,8,256]{2,1,0:T(8,128)S(1)}, u32[]{:S(2)}, u32[]{:S(2)}) %all-to-all-start) | async-done | bytes 131104 | tf_op jit(solution)/shard_map/all_to_all | solution.py:309
  96.5 1.9 %collective-permute-start.9 = (bf16[1,128,256]{2,1,0:T(8,128)(2,1)S(1)}, bf16[1,128,256]{2,1,0:T(8,128)(2,1)S(1)}, u32[]{:S(2)}, u32[]{:S(2)}) collective-permute-start(bf16[1,128,256]{2,1,0:T(8,128)(2,1)S(1)} %dynamic-slice_convert_fusion.2), channel_id=1, source_target_pairs={{0,16},{2,18},{4,20},{6,22},{8,24},{10,26},{12,28},{14,30},{16,0},... | collective-permute-start | bytes 196616 | tf_op jit(solution)/shard_map/ppermute | solution.py:197
  99.0 2.9 %collective-permute-done.9 = bf16[1,128,256]{2,1,0:T(8,128)(2,1)S(1)} collective-permute-done((bf16[1,128,256]{2,1,0:T(8,128)(2,1)S(1)}, bf16[1,128,256]{2,1,0:T(8,128)(2,1)S(1)}, u32[]{:S(2)}, u32[]{:S(2)}) %collective-permute-start.9) | collective-permute-done | bytes 65568 | tf_op jit(solution)/shard_map/ppermute | solution.py:197
  103.5 9.8 %shard_map.208 = bf16[224,4096]{1,0:T(8,128)(2,1)} custom-call(bf16[224,4096]{1,0:T(8,128)(2,1)} %get-tuple-element.30.z_ref, bf16[128,4096]{1,0:T(8,128)(2,1)} %copy-done.1, bf16[224,4096]{1,0:T(8,128)(2,1)} %up_ref.1, f32[128,4096]{1,0:T(8,128)} %f_ref.3, f32[1,4096]{1,0:T(1,128)} %bitcast.36, bf16[352,352]{1,0:T(8,128)(2,1)} %constant.102.clone.fz_ref, ...), custom_call_target="tpu_custom_call" | custom-call | flops 2030043136 | bytes 9162752 | tf_op jit(solution)/shard_map/pallas_call | solution.py:241
  (38 shorter events, 7.3 us)
Async XLA Ops:
  2.4 21.4 %collective-permute-start.2 = (bf16[128,4096]{1,0:T(8,128)(2,1)S(1)}, bf16[128,4096]{1,0:T(8,128)(2,1)S(1)}, u32[]{:S(2)}, u32[]{:S(2)}) collective-permute-start(bf16[128,4096]{1,0:T(8,128)(2,1)S(1)} %multiply_convert_fusion), channel_id=1, source_target_pairs={{2,0},{4,2},{6,4},{8,6},{10,8},{12,10},{14,12},{16,14},{18,16},{20... | collective-permute-start | bytes 3145736 | tf_op jit(solution)/shard_map/ppermute | solution.py:22
  4.7 4.0 %collective-permute-start = (bf16[16,4096]{1,0:T(8,128)(2,1)S(1)}, bf16[16,4096]{1,0:T(8,128)(2,1)S(1)}, u32[]{:S(2)}, u32[]{:S(2)}) collective-permute-start(bf16[16,4096]{1,0:T(8,128)(2,1)S(1)} %multiply_convert_fusion.1), channel_id=1, source_target_pairs={{0,2},{2,4},{4,6},{6,8},{8,10},{10,12},{12,14},{14,16},{16,18},{18... | collective-permute-start | bytes 393224 | tf_op jit(solution)/shard_map/ppermute | solution.py:22
  8.8 0.7 copy-start.2
  17.9 5.9 %collective-permute-start.1 = (f32[224,128]{1,0:T(8,128)}, f32[224,128]{1,0:T(8,128)S(1)}, u32[]{:S(2)}, u32[]{:S(2)}) collective-permute-start(f32[224,128]{1,0:T(8,128)} %get-tuple-element.22.refs_0_), channel_id=1, source_target_pairs={{0,1},{1,0},{2,3},{3,2},{4,5},{5,4},{6,7},{7,6},{8,9},{9,8},{10,11... | collective-permute-start | bytes 344072 | tf_op jit(solution)/shard_map/ppermute | solution.py:207
  23.8 0.6 copy-start.7
  23.9 1.0 copy-start
  40.2 23.2 %copy-start.3 = (f32[4096]{0:T(1024)S(1)}, f32[4096]{0:T(1024)}, u32[]{:S(2)}) copy-start(f32[4096]{0:T(1024)} %param.23) | copy-start | bytes 49156
  40.2 17.8 %collective-permute-start.6 = (bf16[8,128,256]{2,1,0:T(8,128)(2,1)S(1)}, bf16[8,128,256]{2,1,0:T(8,128)(2,1)S(1)}, u32[]{:S(2)}, u32[]{:S(2)}) collective-permute-start(bf16[8,128,256]{2,1,0:T(8,128)(2,1)S(1)} %fusion), channel_id=1, source_target_pairs={{0,2},{2,0},{4,6},{6,4},{8,10},{10,8},{12,14},{14,12},{16,18},{18,... | collective-permute-start | bytes 1572872 | tf_op jit(solution)/shard_map/ppermute | solution.py:197
  50.9 5.3 %collective-permute-start.3 = (f32[224,128]{1,0:T(8,128)}, f32[224,128]{1,0:T(8,128)S(1)}, u32[]{:S(2)}, u32[]{:S(2)}) collective-permute-start(f32[224,128]{1,0:T(8,128)} %get-tuple-element.25.refs_1_), channel_id=1, source_target_pairs={{0,1},{1,0},{2,3},{3,2},{4,5},{5,4},{6,7},{7,6},{8,9},{9,8},{10,11... | collective-permute-start | bytes 344072 | tf_op jit(solution)/shard_map/ppermute | solution.py:207
  56.2 8.3 %copy-start.5 = (f32[224,128]{1,0:T(8,128)}, f32[224,128]{1,0:T(8,128)S(1)}, u32[]{:S(2)}) copy-start(f32[224,128]{1,0:T(8,128)S(1)} %collective-permute-done.3.refs_2_) | copy-start | bytes 344068
  59.4 28.5 %collective-permute-start.7 = (bf16[4,128,256]{2,1,0:T(8,128)(2,1)S(1)}, bf16[4,128,256]{2,1,0:T(8,128)(2,1)S(1)}, u32[]{:S(2)}, u32[]{:S(2)}) collective-permute-start(bf16[4,128,256]{2,1,0:T(8,128)(2,1)S(1)} %fusion.4), channel_id=1, source_target_pairs={{0,4},{2,6},{4,0},{6,2},{8,12},{10,14},{12,8},{14,10},{16,20},{18,... | collective-permute-start | bytes 786440 | tf_op jit(solution)/shard_map/ppermute | solution.py:197
  64.6 4.4 %collective-permute-start.4 = (bf16[16,4096]{1,0:T(8,128)(2,1)S(1)}, bf16[16,4096]{1,0:T(8,128)(2,1)S(1)}, u32[]{:S(2)}, u32[]{:S(2)}) collective-permute-start(bf16[16,4096]{1,0:T(8,128)(2,1)S(1)} %fusion.3), channel_id=1, source_target_pairs={{2,0},{4,2},{6,4},{8,6},{10,8},{12,10},{14,12},{16,14},{18,16},{20... | collective-permute-start | bytes 393224 | tf_op jit(solution)/shard_map/ppermute | solution.py:22
  65.9 36.6 %collective-permute-start.5 = (bf16[128,4096]{1,0:T(8,128)(2,1)}, bf16[128,4096]{1,0:T(8,128)(2,1)S(1)}, u32[]{:S(2)}, u32[]{:S(2)}) collective-permute-start(bf16[128,4096]{1,0:T(8,128)(2,1)} %get-tuple-element.31), channel_id=1, source_target_pairs={{0,2},{2,4},{4,6},{6,8},{8,10},{10,12},{12,14},{14,16},{16,18},{18... | collective-permute-start | bytes 3145736 | tf_op jit(solution)/shard_map/ppermute | solution.py:22
  69.0 0.7 copy-start.6
  82.4 13.9 %all-to-all-start = ((f32[16,8,256]{2,1,0:T(8,128)}), f32[16,8,256]{2,1,0:T(8,128)S(1)}, u32[]{:S(2)}, u32[]{:S(2)}) async-start(f32[16,8,256]{2,1,0:T(8,128)} %get-tuple-element.33), calls=%async_computation | async-start | bytes 262144 | tf_op jit(solution)/shard_map/all_to_all | solution.py:309
  88.0 8.4 %collective-permute-start.8 = (bf16[2,128,256]{2,1,0:T(8,128)(2,1)S(1)}, bf16[2,128,256]{2,1,0:T(8,128)(2,1)S(1)}, u32[]{:S(2)}, u32[]{:S(2)}) collective-permute-start(bf16[2,128,256]{2,1,0:T(8,128)(2,1)S(1)} %fusion.5), channel_id=1, source_target_pairs={{0,8},{2,10},{4,12},{6,14},{8,0},{10,2},{12,4},{14,6},{16,24},{18,... | collective-permute-start | bytes 393224 | tf_op jit(solution)/shard_map/ppermute | solution.py:197
  96.5 5.4 %collective-permute-start.9 = (bf16[1,128,256]{2,1,0:T(8,128)(2,1)S(1)}, bf16[1,128,256]{2,1,0:T(8,128)(2,1)S(1)}, u32[]{:S(2)}, u32[]{:S(2)}) collective-permute-start(bf16[1,128,256]{2,1,0:T(8,128)(2,1)S(1)} %dynamic-slice_convert_fusion.2), channel_id=1, source_target_pairs={{0,16},{2,18},{4,20},{6,22},{8,24},{10,26},{12,28},{14,30},{16,0},... | collective-permute-start | bytes 196616 | tf_op jit(solution)/shard_map/ppermute | solution.py:197
  98.4 14.9 %copy-start.8 = (f32[8,256]{1,0:T(8,128)}, f32[8,256]{1,0:T(8,128)S(1)}, u32[]{:S(2)}) copy-start(f32[8,256]{1,0:T(8,128)S(1)} %broadcast_multiply_fusion) | copy-start | bytes 24580
  101.9 11.4 %copy-start.4 = (f32[1,128,256]{2,1,0:T(8,128)}, f32[1,128,256]{2,1,0:T(8,128)S(1)}, u32[]{:S(2)}) copy-start(f32[1,128,256]{2,1,0:T(8,128)S(1)} %add_multiply_fusion) | copy-start | bytes 393220
  102.5 1.0 copy-start.1

commit v3 on v2

--- a/solution.py
+++ b/solution.py
@@ -57,12 +57,12 @@
 
     for start in range(0, block, LANES):
         cols = slice(start, start + LANES)
-        pad[:halo, :] = tail_ref[:, cols].astype(F32)
+        pad[:halo, cols] = tail_ref[:, cols].astype(F32)
         product = k_ref[:, cols].astype(F32) * v_ref[:, cols].astype(F32)
-        pad[halo:, :] = product.astype(BF16).astype(F32)
-        conv = f_ref[0:1, cols] * pad[pl.ds(halo, rows), :]
+        pad[halo:, cols] = product.astype(BF16).astype(F32)
+        conv = f_ref[0:1, cols] * pad[pl.ds(halo, rows), cols]
         for j in range(1, f_ref.shape[0]):
-            conv = conv + f_ref[j : j + 1, cols] * pad[pl.ds(halo - j, rows), :]
+            conv = conv + f_ref[j : j + 1, cols] * pad[pl.ds(halo - j, rows), cols]
         conv_ref[:, cols] = conv
         mixed = q_ref[:, cols].astype(F32) * conv
         sq_ref[...] += mixed * mixed
@@ -153,21 +153,21 @@
         gm = gain_ref[:, cols] * gn - mixed * coef
         gq_ref[:, cols] = (gm * conv).astype(BF16)
         gc = (gm * q).astype(BF16).astype(F32)
-        pad_g[:rows, :] = gc
-        pad_g[rows:, :] = head_ref[:, cols].astype(F32)
+        pad_g[:rows, cols] = gc
+        pad_g[rows:, cols] = head_ref[:, cols].astype(F32)
         part, inner = start // share, start % share
         place = slice(inner, inner + LANES)
         small_ref[part, taps : taps + 1, place] = jnp.sum(gn * mixed, axis=0, keepdims=True)
         k = k_ref[:, cols].astype(F32)
         v = v_ref[:, cols].astype(F32)
-        pad_p[:halo, :] = tail_ref[:, cols].astype(F32)
-        pad_p[halo:, :] = (k * v).astype(BF16).astype(F32)
+        pad_p[:halo, cols] = tail_ref[:, cols].astype(F32)
+        pad_p[halo:, cols] = (k * v).astype(BF16).astype(F32)
         gp = f_ref[0:1, cols] * gc
         for j in range(taps):
             if j:
-                gp = gp + f_ref[j : j + 1, cols] * pad_g[pl.ds(j, rows), :]
+                gp = gp + f_ref[j : j + 1, cols] * pad_g[pl.ds(j, rows), cols]
             small_ref[part, j : j + 1, place] = jnp.sum(
-                gc * pad_p[pl.ds(halo - j, rows), :], axis=0, keepdims=True
+                gc * pad_p[pl.ds(halo - j, rows), cols], axis=0, keepdims=True
             )
         gk_ref[:, cols] = (gp * v).astype(BF16)
         gv_ref[:, cols] = (gp * k).astype(BF16)
@@ -268,7 +268,7 @@
         (query_se, key_se, value_se, tail_se, filter_se),
         [stream, stream, stream, rowed(halo), rowed(taps_se)],
         [shape(rows, F32), lanes_shape], [stream, lanes_spec],
-        [pltpu.VMEM((halo + rows, LANES), F32)],
+        [pltpu.VMEM((halo + rows, block), F32)],
     )
     sq = exchanged(squares, "tp")
     nsq = len(sq)
@@ -303,7 +303,7 @@
         + [stream, stream, stream, rowed(halo), rowed(halo), stream, stream, one, rowed(taps_se)],
         [shape(rows, BF16)] * 3 + [jax.ShapeDtypeStruct((chans // group, taps_se + 1, group), F32)],
         [stream] * 3 + [pl.BlockSpec((block // group, taps_se + 1, group), lambda i: (i, 0, 0))],
-        [pltpu.VMEM((halo + rows, LANES), F32)] * 2 + [pltpu.VMEM((rows, LANES), F32)],
+        [pltpu.VMEM((halo + rows, block), F32)] * 2 + [pltpu.VMEM((rows, LANES), F32)],
     )
     corr, small = split_parts(corr, share), split_parts(small, share)
     small = lax.all_to_all(small, "ctx", 0, 0, tiled=True)

time: 115 us -> 119 us (1.035)
  Pallas kernels: 45 us -> 49.4 us
    pallas_call x4, Pallas kernels: 45 us -> 49.4 us  [call(): pl.pallas_call(body, grid=(steps,), in_specs=specs, out_specs=out_specs,...]
  transfers between devices with their start and end apart: 11 -> 11, of which waited for: 5 -> 5; matrix products, arithmetic and copies ran while one was open for 5% -> 4% of each run, Pallas kernels for 19% -> 22%
where the time goes in v3:
time: 119 us; the launch traced here: 118 us
  Pallas kernels  49.4 us (42%)
  starting transfers between devices  37.3 us (31%)
  waiting for transfers between devices  17.1 us (14%)
  other arithmetic  7.08 us (6%)
  local copies, waits for them, and re-layouts  5.92 us (5%)
    pallas_call x4, Pallas kernels, call(): pl.pallas_call(body, grid=(steps,), in_specs=specs, out_specs=out_specs,...  49.4 us
    ppermute x4, starting transfers between devices, scatter_sum(): got = lax.ppermute(away, axis, [(i, i ^ bit) for i in range(size)])  18.6 us
    ppermute x4, starting transfers between devices, shifted(): return lax.ppermute(block, axis, route)  8.72 us
    ppermute x2, waiting for transfers between devices, exchanged(): lax.ppermute(value, axis, [(i, (i + step) % size) for i in range(size)])  6.83 us
    all_to_all x1, waiting for transfers between devices, local(): small = lax.all_to_all(small, 'ctx', 0, 0, tiled=True)  6.38 us
    all_to_all x1, starting transfers between devices, local(): small = lax.all_to_all(small, 'ctx', 0, 0, tiled=True)  5.46 us
    ppermute x2, starting transfers between devices, exchanged(): lax.ppermute(value, axis, [(i, (i + step) % size) for i in range(size)])  4.46 us
    unnamed x18, local copies, waits for them, and re-layouts  3.3 us
  transfers between devices with their start and end apart: 11, of which 5 were waited for; matrix products, arithmetic and copies ran while one was open for 4% of the time, Pallas kernels for 22%

profile of v3, /device:TPU:0, one launch (start us, length us, event | category | flops | bytes accessed | tf_op | source)
XLA Modules:
  0.0 117.6 jit_solution(2944080611001929893)
XLA Ops:
  0.6 1.8 %multiply_convert_fusion = bf16[128,4096]{1,0:T(8,128)(2,1)S(1)} fusion(bf16[224,4096]{1,0:T(8,128)(2,1)} %refs_3_.2, bf16[224,4096]{1,0:T(8,128)(2,1)} %up_ref.1), kind=kLoop, calls=%fused_computation | loop fusion | flops 2097152 | bytes 3145728 | tf_op jit(solution)/shard_map/convert_element_type | solution.py:264
  2.4 1.3 %collective-permute-start.2 = (bf16[128,4096]{1,0:T(8,128)(2,1)S(1)}, bf16[128,4096]{1,0:T(8,128)(2,1)S(1)}, u32[]{:S(2)}, u32[]{:S(2)}) collective-permute-start(bf16[128,4096]{1,0:T(8,128)(2,1)S(1)} %multiply_convert_fusion), channel_id=1, source_target_pairs={{2,0},{4,2},{6,4},{8,6},{10,8},{12,10},{14,12},{16,14},{18,16},{20... | collective-permute-start | bytes 3145736 | tf_op jit(solution)/shard_map/ppermute | solution.py:22
  3.7 1.0 multiply_convert_fusion.1
  4.7 3.0 %collective-permute-start = (bf16[16,4096]{1,0:T(8,128)(2,1)S(1)}, bf16[16,4096]{1,0:T(8,128)(2,1)S(1)}, u32[]{:S(2)}, u32[]{:S(2)}) collective-permute-start(bf16[16,4096]{1,0:T(8,128)(2,1)S(1)} %multiply_convert_fusion.1), channel_id=1, source_target_pairs={{0,2},{2,4},{4,6},{6,8},{8,10},{10,12},{12,14},{14,16},{16,18},{18... | collective-permute-start | bytes 393224 | tf_op jit(solution)/shard_map/ppermute | solution.py:22
  9.4 9.3 %shard_map.205 = (f32[224,4096]{1,0:T(8,128)}, f32[224,128]{1,0:T(8,128)}) custom-call(bf16[224,4096]{1,0:T(8,128)(2,1)} %refs_3_.3, bf16[224,4096]{1,0:T(8,128)(2,1)} %refs_4_.1, bf16[224,4096]{1,0:T(8,128)(2,1)} %refs_5_.3, bf16[16,4096]{1,0:T(8,128)(2,1)} %copy-done.2, f32[7,4096]{1,0:T(8,128)} %refs_11_.2), custom_call_target="tpu_custom_call" | custom-call | bytes 9535488 | tf_op jit(solution)/shard_map/pallas_call | solution.py:241
  18.7 3.0 %collective-permute-start.1 = (f32[224,128]{1,0:T(8,128)}, f32[224,128]{1,0:T(8,128)S(1)}, u32[]{:S(2)}, u32[]{:S(2)}) collective-permute-start(f32[224,128]{1,0:T(8,128)} %get-tuple-element.22.refs_0_), channel_id=1, source_target_pairs={{0,1},{1,0},{2,3},{3,2},{4,5},{5,4},{6,7},{7,6},{8,9},{9,8},{10,11... | collective-permute-start | bytes 344072 | tf_op jit(solution)/shard_map/ppermute | solution.py:207
  21.7 3.0 %collective-permute-done.1.refs_1_ = f32[224,128]{1,0:T(8,128)S(1)} collective-permute-done((f32[224,128]{1,0:T(8,128)}, f32[224,128]{1,0:T(8,128)S(1)}, u32[]{:S(2)}, u32[]{:S(2)}) %collective-permute-start.1) | collective-permute-done | bytes 114720 | tf_op jit(solution)/shard_map/ppermute | solution.py:207
  25.7 14.0 %shard_map.206 = (bf16[224,4096]{1,0:T(8,128)(2,1)}, f32[224,4096]{1,0:T(8,128)}, f32[224,128]{1,0:T(8,128)}, bf16[224,4096]{1,0:T(8,128)(2,1)}, bf16[128,4096]{...) custom-call(f32[224,128]{1,0:T(8,128)} %get-tuple-element.22.refs_0_, f32[224,128]{1,0:T(8,128)} %copy-done.7, ...), custom_call_target="tpu_custom_call" | custom-call | flops 3045064704 | bytes 25628672 | tf_op jit(solution)/shard_map/pallas_call | solution.py:241
  39.7 1.3 %fusion = bf16[8,128,256]{2,1,0:T(8,128)(2,1)S(1)} fusion(f32[8,2,128,256]{3,2,1,0:T(8,128)} %bitcast.30, s32[]{:T(128)S(6)} %select_n.41), kind=kLoop, calls=%fused_computation.3 | loop fusion | bytes 1048580 | tf_op jit(solution)/shard_map/convert_element_type | solution.py:195
  41.0 10.7 %collective-permute-start.6 = (bf16[8,128,256]{2,1,0:T(8,128)(2,1)S(1)}, bf16[8,128,256]{2,1,0:T(8,128)(2,1)S(1)}, u32[]{:S(2)}, u32[]{:S(2)}) collective-permute-start(bf16[8,128,256]{2,1,0:T(8,128)(2,1)S(1)} %fusion), channel_id=1, source_target_pairs={{0,2},{2,0},{4,6},{6,4},{8,10},{10,8},{12,14},{14,12},{16,18},{18,... | collective-permute-start | bytes 1572872 | tf_op jit(solution)/shard_map/ppermute | solution.py:197
  51.7 1.5 %collective-permute-start.3 = (f32[224,128]{1,0:T(8,128)}, f32[224,128]{1,0:T(8,128)S(1)}, u32[]{:S(2)}, u32[]{:S(2)}) collective-permute-start(f32[224,128]{1,0:T(8,128)} %get-tuple-element.25.refs_1_), channel_id=1, source_target_pairs={{0,1},{1,0},{2,3},{3,2},{4,5},{5,4},{6,7},{7,6},{8,9},{9,8},{10,11... | collective-permute-start | bytes 344072 | tf_op jit(solution)/shard_map/ppermute | solution.py:207
  53.2 3.9 %collective-permute-done.3.refs_2_ = f32[224,128]{1,0:T(8,128)S(1)} collective-permute-done((f32[224,128]{1,0:T(8,128)}, f32[224,128]{1,0:T(8,128)S(1)}, u32[]{:S(2)}, u32[]{:S(2)}) %collective-permute-start.3) | collective-permute-done | bytes 114720 | tf_op jit(solution)/shard_map/ppermute | solution.py:207
  58.8 1.4 %bitcast_add_fusion = f32[8,128,256]{2,1,0:T(8,128)S(1)} fusion(bf16[8,128,256]{2,1,0:T(8,128)(2,1)S(1)} %collective-permute-done.6, f32[8,2,128,256]{3,2,1,0:T(8,128)} %bitcast.31, s32[]{:T(128)S(6)} %select_n.40), kind=kLoop, calls=%fused_computation.2 | loop fusion | flops 524288 | bytes 2621444 | tf_op jit(solution)/shard_map/add | solution.py:198
  60.2 4.0 %collective-permute-start.7 = (bf16[4,128,256]{2,1,0:T(8,128)(2,1)S(1)}, bf16[4,128,256]{2,1,0:T(8,128)(2,1)S(1)}, u32[]{:S(2)}, u32[]{:S(2)}) collective-permute-start(bf16[4,128,256]{2,1,0:T(8,128)(2,1)S(1)} %fusion.4), channel_id=1, source_target_pairs={{0,4},{2,6},{4,0},{6,2},{8,12},{10,14},{12,8},{14,10},{16,20},{18,... | collective-permute-start | bytes 786440 | tf_op jit(solution)/shard_map/ppermute | solution.py:197
  64.2 1.2 %fusion.3 = bf16[16,4096]{1,0:T(8,128)(2,1)S(1)} fusion(f32[224,4096]{1,0:T(8,128)} %get-tuple-element.23.refs_8_, f32[224,4096]{1,0:T(8,128)} %get-tuple-element.26.refs_9_, f32[16]{0:T(128)S(1)} %get-tuple-element.36, bf16[224,4096]{1,0:T(8,128)(2,1)} %refs_3_.3, f32[16]{0:T(128)S(1)} %get-tuple-element.35, f32[4096]{0:T(1024)S(1)} %copy-done.3), kind=kLoop, calls=%fused_computation.10 | loop fusion | flops 524288 | bytes 802944 | tf_op jit(solution)/shard_map/convert_element_type | solution.py:296
  65.4 1.3 %collective-permute-start.4 = (bf16[16,4096]{1,0:T(8,128)(2,1)S(1)}, bf16[16,4096]{1,0:T(8,128)(2,1)S(1)}, u32[]{:S(2)}, u32[]{:S(2)}) collective-permute-start(bf16[16,4096]{1,0:T(8,128)(2,1)S(1)} %fusion.3), channel_id=1, source_target_pairs={{2,0},{4,2},{6,4},{8,6},{10,8},{12,10},{14,12},{16,14},{18,16},{20... | collective-permute-start | bytes 393224 | tf_op jit(solution)/shard_map/ppermute | solution.py:22
  66.7 3.1 %collective-permute-start.5 = (bf16[128,4096]{1,0:T(8,128)(2,1)}, bf16[128,4096]{1,0:T(8,128)(2,1)S(1)}, u32[]{:S(2)}, u32[]{:S(2)}) collective-permute-start(bf16[128,4096]{1,0:T(8,128)(2,1)} %get-tuple-element.31), channel_id=1, source_target_pairs={{0,2},{2,4},{4,6},{6,8},{8,10},{10,12},{12,14},{14,16},{16,18},{18... | collective-permute-start | bytes 3145736 | tf_op jit(solution)/shard_map/ppermute | solution.py:22
  70.5 16.3 %shard_map.207 = (bf16[224,4096]{1,0:T(8,128)(2,1)}, bf16[224,4096]{1,0:T(8,128)(2,1)}, bf16[224,4096]{1,0:T(8,128)(2,1)}, f32[16,8,256]{2,1,0:T(8,128)}) custom-call(f32[224,128]{1,0:T(8,128)} %get-tuple-element.24.refs_0_, f32[224,128]{1,0:T(8,128)} %get-tuple-element.25.refs_1_, f32[224,128]{1,0:T(8,128)} %copy-done.5, bf16[224,4096]{1,0:T(8,128)(2,1)} %refs_3_.3, ...), custom_call_target="tpu_custom_call" | custom-call | bytes 19218432 | tf_op jit(solution)/shard_map/pallas_call | solution.py:241
  86.8 5.5 %all-to-all-start = ((f32[16,8,256]{2,1,0:T(8,128)}), f32[16,8,256]{2,1,0:T(8,128)S(1)}, u32[]{:S(2)}, u32[]{:S(2)}) async-start(f32[16,8,256]{2,1,0:T(8,128)} %get-tuple-element.33), calls=%async_computation | async-start | bytes 262144 | tf_op jit(solution)/shard_map/all_to_all | solution.py:309
  92.3 2.0 %collective-permute-start.8 = (bf16[2,128,256]{2,1,0:T(8,128)(2,1)S(1)}, bf16[2,128,256]{2,1,0:T(8,128)(2,1)S(1)}, u32[]{:S(2)}, u32[]{:S(2)}) collective-permute-start(bf16[2,128,256]{2,1,0:T(8,128)(2,1)S(1)} %fusion.5), channel_id=1, source_target_pairs={{0,8},{2,10},{4,12},{6,14},{8,0},{10,2},{12,4},{14,6},{16,24},{18,... | collective-permute-start | bytes 393224 | tf_op jit(solution)/shard_map/ppermute | solution.py:197
  94.3 6.4 %all-to-all-done = f32[16,8,256]{2,1,0:T(8,128)S(1)} async-done(((f32[16,8,256]{2,1,0:T(8,128)}), f32[16,8,256]{2,1,0:T(8,128)S(1)}, u32[]{:S(2)}, u32[]{:S(2)}) %all-to-all-start) | async-done | bytes 131104 | tf_op jit(solution)/shard_map/all_to_all | solution.py:309
  100.8 1.9 %collective-permute-start.9 = (bf16[1,128,256]{2,1,0:T(8,128)(2,1)S(1)}, bf16[1,128,256]{2,1,0:T(8,128)(2,1)S(1)}, u32[]{:S(2)}, u32[]{:S(2)}) collective-permute-start(bf16[1,128,256]{2,1,0:T(8,128)(2,1)S(1)} %dynamic-slice_convert_fusion.2), channel_id=1, source_target_pairs={{0,16},{2,18},{4,20},{6,22},{8,24},{10,26},{12,28},{14,30},{16,0},... | collective-permute-start | bytes 196616 | tf_op jit(solution)/shard_map/ppermute | solution.py:197
  103.3 2.9 %collective-permute-done.9 = bf16[1,128,256]{2,1,0:T(8,128)(2,1)S(1)} collective-permute-done((bf16[1,128,256]{2,1,0:T(8,128)(2,1)S(1)}, bf16[1,128,256]{2,1,0:T(8,128)(2,1)S(1)}, u32[]{:S(2)}, u32[]{:S(2)}) %collective-permute-start.9) | collective-permute-done | bytes 65568 | tf_op jit(solution)/shard_map/ppermute | solution.py:197
  107.8 9.8 %shard_map.208 = bf16[224,4096]{1,0:T(8,128)(2,1)} custom-call(bf16[224,4096]{1,0:T(8,128)(2,1)} %get-tuple-element.30.z_ref, bf16[128,4096]{1,0:T(8,128)(2,1)} %copy-done.1, bf16[224,4096]{1,0:T(8,128)(2,1)} %up_ref.1, f32[128,4096]{1,0:T(8,128)} %f_ref.3, f32[1,4096]{1,0:T(1,128)} %bitcast.36, bf16[352,352]{1,0:T(8,128)(2,1)} %constant.102.clone.fz_ref, ...), custom_call_target="tpu_custom_call" | custom-call | flops 2030043136 | bytes 9162752 | tf_op jit(solution)/shard_map/pallas_call | solution.py:241
  (38 shorter events, 7.3 us)
Async XLA Ops:
  2.4 22.2 %collective-permute-start.2 = (bf16[128,4096]{1,0:T(8,128)(2,1)S(1)}, bf16[128,4096]{1,0:T(8,128)(2,1)S(1)}, u32[]{:S(2)}, u32[]{:S(2)}) collective-permute-start(bf16[128,4096]{1,0:T(8,128)(2,1)S(1)} %multiply_convert_fusion), channel_id=1, source_target_pairs={{2,0},{4,2},{6,4},{8,6},{10,8},{12,10},{14,12},{16,14},{18,16},{20... | collective-permute-start | bytes 3145736 | tf_op jit(solution)/shard_map/ppermute | solution.py:22
  4.7 4.0 %collective-permute-start = (bf16[16,4096]{1,0:T(8,128)(2,1)S(1)}, bf16[16,4096]{1,0:T(8,128)(2,1)S(1)}, u32[]{:S(2)}, u32[]{:S(2)}) collective-permute-start(bf16[16,4096]{1,0:T(8,128)(2,1)S(1)} %multiply_convert_fusion.1), channel_id=1, source_target_pairs={{0,2},{2,4},{4,6},{6,8},{8,10},{10,12},{12,14},{14,16},{16,18},{18... | collective-permute-start | bytes 393224 | tf_op jit(solution)/shard_map/ppermute | solution.py:22
  8.8 0.7 copy-start.2
  18.7 5.9 %collective-permute-start.1 = (f32[224,128]{1,0:T(8,128)}, f32[224,128]{1,0:T(8,128)S(1)}, u32[]{:S(2)}, u32[]{:S(2)}) collective-permute-start(f32[224,128]{1,0:T(8,128)} %get-tuple-element.22.refs_0_), channel_id=1, source_target_pairs={{0,1},{1,0},{2,3},{3,2},{4,5},{5,4},{6,7},{7,6},{8,9},{9,8},{10,11... | collective-permute-start | bytes 344072 | tf_op jit(solution)/shard_map/ppermute | solution.py:207
  24.7 0.6 copy-start.7
  24.7 1.0 copy-start
  41.0 23.2 %copy-start.3 = (f32[4096]{0:T(1024)S(1)}, f32[4096]{0:T(1024)}, u32[]{:S(2)}) copy-start(f32[4096]{0:T(1024)} %param.23) | copy-start | bytes 49156
  41.0 17.8 %collective-permute-start.6 = (bf16[8,128,256]{2,1,0:T(8,128)(2,1)S(1)}, bf16[8,128,256]{2,1,0:T(8,128)(2,1)S(1)}, u32[]{:S(2)}, u32[]{:S(2)}) collective-permute-start(bf16[8,128,256]{2,1,0:T(8,128)(2,1)S(1)} %fusion), channel_id=1, source_target_pairs={{0,2},{2,0},{4,6},{6,4},{8,10},{10,8},{12,14},{14,12},{16,18},{18,... | collective-permute-start | bytes 1572872 | tf_op jit(solution)/shard_map/ppermute | solution.py:197
  51.7 5.3 %collective-permute-start.3 = (f32[224,128]{1,0:T(8,128)}, f32[224,128]{1,0:T(8,128)S(1)}, u32[]{:S(2)}, u32[]{:S(2)}) collective-permute-start(f32[224,128]{1,0:T(8,128)} %get-tuple-element.25.refs_1_), channel_id=1, source_target_pairs={{0,1},{1,0},{2,3},{3,2},{4,5},{5,4},{6,7},{7,6},{8,9},{9,8},{10,11... | collective-permute-start | bytes 344072 | tf_op jit(solution)/shard_map/ppermute | solution.py:207
  57.1 8.3 %copy-start.5 = (f32[224,128]{1,0:T(8,128)}, f32[224,128]{1,0:T(8,128)S(1)}, u32[]{:S(2)}) copy-start(f32[224,128]{1,0:T(8,128)S(1)} %collective-permute-done.3.refs_2_) | copy-start | bytes 344068
  60.2 32.0 %collective-permute-start.7 = (bf16[4,128,256]{2,1,0:T(8,128)(2,1)S(1)}, bf16[4,128,256]{2,1,0:T(8,128)(2,1)S(1)}, u32[]{:S(2)}, u32[]{:S(2)}) collective-permute-start(bf16[4,128,256]{2,1,0:T(8,128)(2,1)S(1)} %fusion.4), channel_id=1, source_target_pairs={{0,4},{2,6},{4,0},{6,2},{8,12},{10,14},{12,8},{14,10},{16,20},{18,... | collective-permute-start | bytes 786440 | tf_op jit(solution)/shard_map/ppermute | solution.py:197
  65.4 4.4 %collective-permute-start.4 = (bf16[16,4096]{1,0:T(8,128)(2,1)S(1)}, bf16[16,4096]{1,0:T(8,128)(2,1)S(1)}, u32[]{:S(2)}, u32[]{:S(2)}) collective-permute-start(bf16[16,4096]{1,0:T(8,128)(2,1)S(1)} %fusion.3), channel_id=1, source_target_pairs={{2,0},{4,2},{6,4},{8,6},{10,8},{12,10},{14,12},{16,14},{18,16},{20... | collective-permute-start | bytes 393224 | tf_op jit(solution)/shard_map/ppermute | solution.py:22
  66.7 40.1 %collective-permute-start.5 = (bf16[128,4096]{1,0:T(8,128)(2,1)}, bf16[128,4096]{1,0:T(8,128)(2,1)S(1)}, u32[]{:S(2)}, u32[]{:S(2)}) collective-permute-start(bf16[128,4096]{1,0:T(8,128)(2,1)} %get-tuple-element.31), channel_id=1, source_target_pairs={{0,2},{2,4},{4,6},{6,8},{8,10},{10,12},{12,14},{14,16},{16,18},{18... | collective-permute-start | bytes 3145736 | tf_op jit(solution)/shard_map/ppermute | solution.py:22
  69.8 0.7 copy-start.6
  86.8 13.9 %all-to-all-start = ((f32[16,8,256]{2,1,0:T(8,128)}), f32[16,8,256]{2,1,0:T(8,128)S(1)}, u32[]{:S(2)}, u32[]{:S(2)}) async-start(f32[16,8,256]{2,1,0:T(8,128)} %get-tuple-element.33), calls=%async_computation | async-start | bytes 262144 | tf_op jit(solution)/shard_map/all_to_all | solution.py:309
  92.3 8.4 %collective-permute-start.8 = (bf16[2,128,256]{2,1,0:T(8,128)(2,1)S(1)}, bf16[2,128,256]{2,1,0:T(8,128)(2,1)S(1)}, u32[]{:S(2)}, u32[]{:S(2)}) collective-permute-start(bf16[2,128,256]{2,1,0:T(8,128)(2,1)S(1)} %fusion.5), channel_id=1, source_target_pairs={{0,8},{2,10},{4,12},{6,14},{8,0},{10,2},{12,4},{14,6},{16,24},{18,... | collective-permute-start | bytes 393224 | tf_op jit(solution)/shard_map/ppermute | solution.py:197
  100.8 5.4 %collective-permute-start.9 = (bf16[1,128,256]{2,1,0:T(8,128)(2,1)S(1)}, bf16[1,128,256]{2,1,0:T(8,128)(2,1)S(1)}, u32[]{:S(2)}, u32[]{:S(2)}) collective-permute-start(bf16[1,128,256]{2,1,0:T(8,128)(2,1)S(1)} %dynamic-slice_convert_fusion.2), channel_id=1, source_target_pairs={{0,16},{2,18},{4,20},{6,22},{8,24},{10,26},{12,28},{14,30},{16,0},... | collective-permute-start | bytes 196616 | tf_op jit(solution)/shard_map/ppermute | solution.py:197
  102.7 14.9 %copy-start.8 = (f32[8,256]{1,0:T(8,128)}, f32[8,256]{1,0:T(8,128)S(1)}, u32[]{:S(2)}) copy-start(f32[8,256]{1,0:T(8,128)S(1)} %broadcast_multiply_fusion) | copy-start | bytes 24580
  106.2 11.4 %copy-start.4 = (f32[1,128,256]{2,1,0:T(8,128)}, f32[1,128,256]{2,1,0:T(8,128)S(1)}, u32[]{:S(2)}) copy-start(f32[1,128,256]{2,1,0:T(8,128)S(1)} %add_multiply_fusion) | copy-start | bytes 393220
  106.8 1.0 copy-start.1
